TPU v7x, 8 devices: a whole 2x2x1 slice. The times are simulated.
8 devices in a mesh: data: 1 (over z), dap: 8 (over y, x, core).
Axes of the slice: x: 2, y: 2, z: 1, core: 2. Of those that a mesh axis runs over, the one named last changes fastest.
Arguments:
- extra_msa: bfloat16 [3072, 256, 64], P('data', 'dap')
- extra_mask: int32 [3072, 256], P('data')
- main_msa: bfloat16 [256, 256, 256], P('data', 'dap')
- main_mask: int32 [256, 256], P('data')
- pair_act: float32 [256, 256, 128], P(('data', 'dap'))
- extra_ln_gamma: bfloat16 [64], replicated
- extra_ln_beta: bfloat16 [64], replicated
- extra_w_left: bfloat16 [64, 32], replicated
- extra_b_left: bfloat16 [32], replicated
- extra_w_right: bfloat16 [64, 32], replicated
- extra_b_right: bfloat16 [32], replicated
- extra_w_out: bfloat16 [1024, 128], replicated
- extra_b_out: bfloat16 [128], replicated
- main_ln_gamma: bfloat16 [256], replicated
- main_ln_beta: bfloat16 [256], replicated
- main_w_left: bfloat16 [256, 32], replicated
- main_b_left: bfloat16 [32], replicated
- main_w_right: bfloat16 [256, 32], replicated
- main_b_right: bfloat16 [32], replicated
- main_w_out: bfloat16 [1024, 128], replicated
- main_b_out: bfloat16 [128], replicated
Outputs:
- output 1: float32 [256, 256, 128], P(('data', 'dap'))
- output 2: bfloat16 [3072, 256, 64], P(('data', 'dap'))
- output 3: bfloat16 [256, 256, 256], P(('data', 'dap'))
All inputs are finite; a program needn't handle non-finite values.
Results may differ from a plain program's by a relative error of at most 0.00470469.
Values are sent between devices in bfloat16 or wider.
A program may use at most 1 GiB of HBM per device.

v0:
```python
import jax
import jax.numpy as jnp
from jax import lax
from jax.sharding import PartitionSpec as P

LN_EPS = 1e-5
NORM_EPS = 1e-3


def layer_norm(value_a10, ln_gamma, ln_beta):
    as_float = value_a10.astype(jnp.float32)
    row_mean = jnp.mean(as_float, axis=-1, keepdims=True)
    centered = as_float - row_mean
    row_var = jnp.mean(centered * centered, axis=-1, keepdims=True)
    scaled = centered * lax.rsqrt(row_var + LN_EPS)
    return (scaled * ln_gamma.astype(jnp.float32) + ln_beta.astype(jnp.float32)).astype(jnp.bfloat16)


def project_pair(normed, mask_float, w_left, b_left, w_right, b_right):
    hidden = w_left.shape[1]
    w_both = jnp.concatenate([w_left, w_right], axis=1)
    b_both = jnp.concatenate([b_left, b_right]).astype(jnp.float32)
    both_proj = jnp.einsum('...m,mc->...c', normed, w_both, preferred_element_type=jnp.float32)
    both_proj = ((both_proj + b_both) * mask_float[..., None]).astype(jnp.bfloat16)
    return both_proj[..., :hidden], both_proj[..., hidden:]


def pair_counts(mask_rows, mask_full):
    return jnp.einsum('si,sj->ij', mask_rows.astype(jnp.bfloat16), mask_full.astype(jnp.bfloat16), preferred_element_type=jnp.float32)


def gathered_term(value_a9, mask_full, ln_gamma, ln_beta, w_left, b_left, w_right, b_right, w_out, b_out):
    row_count = value_a9.shape[1]
    hidden = w_left.shape[1]
    row_start = lax.axis_index('dap') * row_count
    mask_rows = lax.dynamic_slice_in_dim(mask_full, row_start, row_count, axis=1)
    normed = layer_norm(value_a9, ln_gamma, ln_beta)
    left_proj, right_proj = project_pair(normed, mask_rows.astype(jnp.float32), w_left, b_left, w_right, b_right)
    right_all = lax.all_gather(right_proj, 'dap', axis=1, tiled=True)
    outer_prod = jnp.einsum('sic,sjd->ijcd', left_proj, right_all, preferred_element_type=jnp.float32).astype(jnp.bfloat16)
    pair_sum = jnp.einsum('ijcd,cdk->ijk', outer_prod, w_out.reshape(hidden, hidden, -1), preferred_element_type=jnp.float32)
    counts = pair_counts(mask_rows, mask_full)
    return (pair_sum + b_out.astype(jnp.float32)) / (NORM_EPS + counts)[:, :, None]


def reduced_term(relaid, mask_full, dap_size, ln_gamma, ln_beta, w_left, b_left, w_right, b_right, w_out, b_out):
    seq_local, res_count, array_b9 = relaid.shape
    hidden = w_left.shape[1]
    row_count = res_count // dap_size
    dap_index = lax.axis_index('dap')
    mask_local = lax.dynamic_slice_in_dim(mask_full, dap_index * seq_local, seq_local, axis=0)
    normed = layer_norm(relaid, ln_gamma, ln_beta)
    left_proj, right_proj = project_pair(normed, mask_local.astype(jnp.float32), w_left, b_left, w_right, b_right)
    left_blocks = jnp.moveaxis(left_proj.reshape(seq_local, dap_size, row_count, hidden), 1, 0)
    w_grid = w_out.reshape(hidden, hidden, -1)

    def block_partial(left_block):
        outer_prod = jnp.einsum('sic,sjd->ijcd', left_block, right_proj, preferred_element_type=jnp.float32).astype(jnp.bfloat16)
        return jnp.einsum('ijcd,cdk->ijk', outer_prod, w_grid, preferred_element_type=jnp.float32).astype(jnp.bfloat16)

    partial_sums = lax.map(block_partial, left_blocks).reshape(res_count, res_count, -1)
    reduced = lax.psum_scatter(partial_sums, 'dap', scatter_dimension=0, tiled=True)
    mask_rows = lax.dynamic_slice_in_dim(mask_full, dap_index * row_count, row_count, axis=1)
    counts = pair_counts(mask_rows, mask_full)
    return (reduced.astype(jnp.float32) + b_out.astype(jnp.float32)) / (NORM_EPS + counts)[:, :, None]


def solution(mesh):
    dap_size = mesh.shape['dap']
    value_a8 = P('data', 'dap', None)
    mask_spec = P('data', None)
    row_spec = P(('data', 'dap'), None, None)

    def local_program(extra_block, extra_mask, main_block, main_mask, pair_rows, extra_ln_gamma, extra_ln_beta, extra_w_left, extra_b_left, extra_w_right, extra_b_right, extra_w_out, extra_b_out, main_ln_gamma, main_ln_beta, main_w_left, main_b_left, main_w_right, main_b_right, main_w_out, main_b_out):
        extra_relaid = lax.all_to_all(extra_block, 'dap', 0, 1, tiled=True)
        extra_term = reduced_term(extra_relaid, extra_mask, dap_size, extra_ln_gamma, extra_ln_beta, extra_w_left, extra_b_left, extra_w_right, extra_b_right, extra_w_out, extra_b_out)
        main_term = gathered_term(main_block, main_mask, main_ln_gamma, main_ln_beta, main_w_left, main_b_left, main_w_right, main_b_right, main_w_out, main_b_out)
        main_relaid = lax.all_to_all(main_block, 'dap', 0, 1, tiled=True)
        return pair_rows + extra_term + main_term, extra_relaid, main_relaid

    in_specs = (value_a8, mask_spec, value_a8, mask_spec, row_spec) + (P(),) * 16
    sharded = jax.shard_map(local_program, mesh=mesh, in_specs=in_specs, out_specs=(row_spec, row_spec, row_spec), check_vma=False)
    return sharded
```

profile of v0, /device:TPU:0, one launch (start us, length us, event | category | flops | bytes accessed | tf_op | source)
XLA Modules:
  0.0 801.8 jit_solution(10163902019694493975)
XLA Ops:
  7.2 0.0 copy-start
  7.2 35.0 %copy.76 = bf16[3072,32,64]{2,1,0:T(8,128)(2,1)} copy(bf16[3072,32,64]{0,2,1:T(8,128)(2,1)} %param.23) | data formatting | bytes 25165824 | tf_op args[0]
  42.2 22.7 %reshape.113 = bf16[8,2,393216]{2,1,0:T(2,128)(2,1)} reshape(bf16[3072,32,64]{2,1,0:T(8,128)(2,1)} %copy.76) | data formatting | bytes 25165824
  64.9 4.3 all-to-all-start
  69.2 0.0 all-gather.2.cloned.1.call-start
  69.2 0.1 constant_dynamic-slice_fusion
  69.4 0.1 copy.96
  69.4 0.0 copy-start.1
  69.5 0.1 maximum_convert_fusion.1
  69.6 3.5 convert_reduce_fusion.1
  73.1 4.0 fusion.17
  77.1 0.0 copy-start.8
  77.2 3.1 fusion.20
  80.3 2.6 multiply_convert_fusion.1
  82.9 1.0 copy-done.3
  83.9 0.8 slice.18
  84.7 0.0 all-gather.2.cloned.1.call-update
  84.7 0.0 reduce-scatter.2.cloned.1.call-start
  84.8 0.1 copy.84
  85.0 0.1 maximum_convert_fusion
  85.0 1.0 dynamic-slice_convert_fusion.2
  86.1 140.0 %all-to-all-done = bf16[8,2,393216]{2,1,0:T(2,128)(2,1)} async-done(((bf16[8,2,393216]{2,1,0:T(2,128)(2,1)}), bf16[8,2,393216]{2,1,0:T(2,128)(2,1)}, u32[]{:S(2)}, u32[]{:S(2)}) %all-to-all-start) | async-done | bytes 12582944 | tf_op jit(solution)/shard_map/all_to_all | solution.py:75
  226.0 22.6 %reshape.114 = bf16[3072,32,64]{2,1,0:T(8,128)(2,1)} reshape(bf16[8,2,393216]{2,1,0:T(2,128)(2,1)} %all-to-all-done) | data formatting | bytes 25165824
  248.7 23.9 %copy.94 = bf16[8,384,32,64]{1,0,3,2:T(8,128)(2,1)} copy(bf16[8,384,32,64]{3,2,1,0:T(8,128)(2,1)} %bitcast.91) | data formatting | bytes 25165824 | tf_op jit(solution)/shard_map/all_to_all | solution.py:75
  272.6 6.5 convert_reduce_fusion
  279.2 8.5 %fusion.14 = f32[384,8,32]{0,1,2:T(8,128)S(1)} fusion(bf16[8,384,32,64]{1,0,3,2:T(8,128)(2,1)} %copy.94, f32[384,8,32]{0,1,2:T(8,128)S(1)} %broadcast_multiply_fusion), kind=kLoop, calls=%fused_computation.15 | loop fusion | flops 25067520 | bytes 13369344 | tf_op jit(solution)/shard_map/reduce_sum | solution.py:14
  287.7 0.1 copy.79
  287.8 0.1 add_rsqrt_fusion
  287.8 0.1 copy.80
  287.9 31.3 %copy.78 = bf16[384,8,32,64]{0,3,2,1:T(8,128)(2,1)} copy(bf16[384,8,32,64]{3,2,0,1:T(8,128)(2,1)} %bitcast.92) | data formatting | bytes 25165824 | tf_op jit(solution)/shard_map/all_to_all | solution.py:75
  319.2 12.9 %add_convert_fusion = bf16[384,256,64]{0,2,1:T(8,128)(2,1)} fusion(f32[64]{0:T(128)S(1)} %convert_element_type.93, f32[64]{0:T(128)S(1)} %convert_element_type.92, f32[384,256]{0,1:T(8,128)S(1)} %bitcast.98, f32[384,256]{0,1:T(8,128)S(1)} %bitcast.97, bf16[384,8,32,64]{0,3,2,1:T(8,128)(2,1)} %copy.78), kind=kLoop, calls=%fused_computation.17 | loop fusion | flops 37748736 | bytes 25952768 | tf_op jit(solution)/shard_map/convert_element_type | solution.py:16
  332.1 18.2 %copy.81 = bf16[384,256,64]{1,2,0:T(8,128)(2,1)} copy(bf16[384,256,64]{0,2,1:T(8,128)(2,1)} %add_convert_fusion) | data formatting | bytes 25165824 | tf_op jit(solution)/shard_map/convert_element_type | solution.py:16
  350.2 6.6 multiply_convert_fusion
  356.9 5.2 fusion.42
  362.1 9.8 %copy.82 = bf16[384,256,32]{0,2,1:T(8,128)(2,1)} copy(bf16[384,256,32]{1,2,0:T(8,128)(2,1)} %get-tuple-element.87) | data formatting | bytes 12582912 | tf_op jit(solution)/shard_map/slice | solution.py:25
  371.8 8.9 %copy.83 = bf16[384,256,32]{1,0,2:T(8,128)(2,1)} copy(bf16[384,256,32]{1,2,0:T(8,128)(2,1)} %get-tuple-element.86) | data formatting | bytes 12582912 | tf_op jit(solution)/shard_map/while | solution.py:61
  380.8 193.1 %while.10 = (s32[]{:T(128)}, bf16[8,32,256,128]{3,2,1,0:T(8,128)(2,1)}, bf16[8,384,32,32]{1,3,2,0:T(8,128)(2,1)}, bf16[384,256,32]{1,0,2:T(8,128)(2,1)}, bf16[32,32,128]{2,0,1:T(8,128)(2,1)S(1)}, /*index=5*/s32[]{:T(128)}) while((s32[]{:T(128)}, bf16[8,32,256,128]{3,2,1,0:T(8,128)(2,1)}, bf16[8,384,32,32]{1,3,2,0:T(8,128)(2,1)}, ...), condition=%wide.region_3.4_spmd, body=%wide.region_2.3_spmd.sunk | while | flops 8590983168 | bytes 42992708 | solution.py:61
  380.8 14.4 %fusion.56 = bf16[32,32,256,32]{2,1,3,0:T(8,128)(2,1)} fusion(bf16[384,256,32]{1,0,2:T(8,128)(2,1)} %get-tuple-element.134, bf16[8,384,32,32]{1,3,2,0:T(8,128)(2,1)} %get-tuple-element.133, s32[]{:T(128)} %get-tuple-element.125), kind=kOutput, calls=%fused_computation.3.clone.1 | convolution fusion | flops 6442450944 | bytes 23855616 | tf_op jit(solution)/shard_map/while/body/eval_jaxpr/sic,sjd->ijcd/dot_general | solution.py:58
  395.2 9.7 %bitcast_dynamic-update-slice_fusion.2 = bf16[8,32,256,128]{3,2,1,0:T(8,128)(2,1)} fusion(bf16[8,32,256,128]{3,2,1,0:T(8,128)(2,1)} %get-tuple-element.126, s32[]{:T(128)} %get-tuple-element.125, bf16[32,32,256,32]{2,1,3,0:T(8,128)(2,1)} %fusion.56, bf16[32,32,128]{2,0,1:T(8,128)(2,1)S(1)} %get-tuple-element.135), kind=kOutput, calls=%fused_computation.6.clone.1 | convolution fusion | flops 2148532224 | bytes 19137024 | tf_op jit(solution)/shard_map/while/body/eval_jaxpr/ijcd,cdk->ijk/dot_general | solution.py:59
  404.9 14.4 %fusion.56 = bf16[32,32,256,32]{2,1,3,0:T(8,128)(2,1)} fusion(bf16[384,256,32]{1,0,2:T(8,128)(2,1)} %get-tuple-element.134, bf16[8,384,32,32]{1,3,2,0:T(8,128)(2,1)} %get-tuple-element.133, s32[]{:T(128)} %get-tuple-element.125), kind=kOutput, calls=%fused_computation.3.clone.1 | convolution fusion | flops 6442450944 | bytes 23855616 | tf_op jit(solution)/shard_map/while/body/eval_jaxpr/sic,sjd->ijcd/dot_general | solution.py:58
  419.3 9.7 %bitcast_dynamic-update-slice_fusion.2 = bf16[8,32,256,128]{3,2,1,0:T(8,128)(2,1)} fusion(bf16[8,32,256,128]{3,2,1,0:T(8,128)(2,1)} %get-tuple-element.126, s32[]{:T(128)} %get-tuple-element.125, bf16[32,32,256,32]{2,1,3,0:T(8,128)(2,1)} %fusion.56, bf16[32,32,128]{2,0,1:T(8,128)(2,1)S(1)} %get-tuple-element.135), kind=kOutput, calls=%fused_computation.6.clone.1 | convolution fusion | flops 2148532224 | bytes 19137024 | tf_op jit(solution)/shard_map/while/body/eval_jaxpr/ijcd,cdk->ijk/dot_general | solution.py:59
  429.1 14.4 %fusion.56 = bf16[32,32,256,32]{2,1,3,0:T(8,128)(2,1)} fusion(bf16[384,256,32]{1,0,2:T(8,128)(2,1)} %get-tuple-element.134, bf16[8,384,32,32]{1,3,2,0:T(8,128)(2,1)} %get-tuple-element.133, s32[]{:T(128)} %get-tuple-element.125), kind=kOutput, calls=%fused_computation.3.clone.1 | convolution fusion | flops 6442450944 | bytes 23855616 | tf_op jit(solution)/shard_map/while/body/eval_jaxpr/sic,sjd->ijcd/dot_general | solution.py:58
  443.5 9.7 %bitcast_dynamic-update-slice_fusion.2 = bf16[8,32,256,128]{3,2,1,0:T(8,128)(2,1)} fusion(bf16[8,32,256,128]{3,2,1,0:T(8,128)(2,1)} %get-tuple-element.126, s32[]{:T(128)} %get-tuple-element.125, bf16[32,32,256,32]{2,1,3,0:T(8,128)(2,1)} %fusion.56, bf16[32,32,128]{2,0,1:T(8,128)(2,1)S(1)} %get-tuple-element.135), kind=kOutput, calls=%fused_computation.6.clone.1 | convolution fusion | flops 2148532224 | bytes 19137024 | tf_op jit(solution)/shard_map/while/body/eval_jaxpr/ijcd,cdk->ijk/dot_general | solution.py:59
  453.2 14.4 %fusion.56 = bf16[32,32,256,32]{2,1,3,0:T(8,128)(2,1)} fusion(bf16[384,256,32]{1,0,2:T(8,128)(2,1)} %get-tuple-element.134, bf16[8,384,32,32]{1,3,2,0:T(8,128)(2,1)} %get-tuple-element.133, s32[]{:T(128)} %get-tuple-element.125), kind=kOutput, calls=%fused_computation.3.clone.1 | convolution fusion | flops 6442450944 | bytes 23855616 | tf_op jit(solution)/shard_map/while/body/eval_jaxpr/sic,sjd->ijcd/dot_general | solution.py:58
  467.6 9.7 %bitcast_dynamic-update-slice_fusion.2 = bf16[8,32,256,128]{3,2,1,0:T(8,128)(2,1)} fusion(bf16[8,32,256,128]{3,2,1,0:T(8,128)(2,1)} %get-tuple-element.126, s32[]{:T(128)} %get-tuple-element.125, bf16[32,32,256,32]{2,1,3,0:T(8,128)(2,1)} %fusion.56, bf16[32,32,128]{2,0,1:T(8,128)(2,1)S(1)} %get-tuple-element.135), kind=kOutput, calls=%fused_computation.6.clone.1 | convolution fusion | flops 2148532224 | bytes 19137024 | tf_op jit(solution)/shard_map/while/body/eval_jaxpr/ijcd,cdk->ijk/dot_general | solution.py:59
  477.3 14.4 %fusion.56 = bf16[32,32,256,32]{2,1,3,0:T(8,128)(2,1)} fusion(bf16[384,256,32]{1,0,2:T(8,128)(2,1)} %get-tuple-element.134, bf16[8,384,32,32]{1,3,2,0:T(8,128)(2,1)} %get-tuple-element.133, s32[]{:T(128)} %get-tuple-element.125), kind=kOutput, calls=%fused_computation.3.clone.1 | convolution fusion | flops 6442450944 | bytes 23855616 | tf_op jit(solution)/shard_map/while/body/eval_jaxpr/sic,sjd->ijcd/dot_general | solution.py:58
  491.7 9.7 %bitcast_dynamic-update-slice_fusion.2 = bf16[8,32,256,128]{3,2,1,0:T(8,128)(2,1)} fusion(bf16[8,32,256,128]{3,2,1,0:T(8,128)(2,1)} %get-tuple-element.126, s32[]{:T(128)} %get-tuple-element.125, bf16[32,32,256,32]{2,1,3,0:T(8,128)(2,1)} %fusion.56, bf16[32,32,128]{2,0,1:T(8,128)(2,1)S(1)} %get-tuple-element.135), kind=kOutput, calls=%fused_computation.6.clone.1 | convolution fusion | flops 2148532224 | bytes 19137024 | tf_op jit(solution)/shard_map/while/body/eval_jaxpr/ijcd,cdk->ijk/dot_general | solution.py:59
  501.5 14.4 %fusion.56 = bf16[32,32,256,32]{2,1,3,0:T(8,128)(2,1)} fusion(bf16[384,256,32]{1,0,2:T(8,128)(2,1)} %get-tuple-element.134, bf16[8,384,32,32]{1,3,2,0:T(8,128)(2,1)} %get-tuple-element.133, s32[]{:T(128)} %get-tuple-element.125), kind=kOutput, calls=%fused_computation.3.clone.1 | convolution fusion | flops 6442450944 | bytes 23855616 | tf_op jit(solution)/shard_map/while/body/eval_jaxpr/sic,sjd->ijcd/dot_general | solution.py:58
  515.9 9.7 %bitcast_dynamic-update-slice_fusion.2 = bf16[8,32,256,128]{3,2,1,0:T(8,128)(2,1)} fusion(bf16[8,32,256,128]{3,2,1,0:T(8,128)(2,1)} %get-tuple-element.126, s32[]{:T(128)} %get-tuple-element.125, bf16[32,32,256,32]{2,1,3,0:T(8,128)(2,1)} %fusion.56, bf16[32,32,128]{2,0,1:T(8,128)(2,1)S(1)} %get-tuple-element.135), kind=kOutput, calls=%fused_computation.6.clone.1 | convolution fusion | flops 2148532224 | bytes 19137024 | tf_op jit(solution)/shard_map/while/body/eval_jaxpr/ijcd,cdk->ijk/dot_general | solution.py:59
  525.6 14.4 %fusion.56 = bf16[32,32,256,32]{2,1,3,0:T(8,128)(2,1)} fusion(bf16[384,256,32]{1,0,2:T(8,128)(2,1)} %get-tuple-element.134, bf16[8,384,32,32]{1,3,2,0:T(8,128)(2,1)} %get-tuple-element.133, s32[]{:T(128)} %get-tuple-element.125), kind=kOutput, calls=%fused_computation.3.clone.1 | convolution fusion | flops 6442450944 | bytes 23855616 | tf_op jit(solution)/shard_map/while/body/eval_jaxpr/sic,sjd->ijcd/dot_general | solution.py:58
  540.0 9.8 %bitcast_dynamic-update-slice_fusion.2 = bf16[8,32,256,128]{3,2,1,0:T(8,128)(2,1)} fusion(bf16[8,32,256,128]{3,2,1,0:T(8,128)(2,1)} %get-tuple-element.126, s32[]{:T(128)} %get-tuple-element.125, bf16[32,32,256,32]{2,1,3,0:T(8,128)(2,1)} %fusion.56, bf16[32,32,128]{2,0,1:T(8,128)(2,1)S(1)} %get-tuple-element.135), kind=kOutput, calls=%fused_computation.6.clone.1 | convolution fusion | flops 2148532224 | bytes 19137024 | tf_op jit(solution)/shard_map/while/body/eval_jaxpr/ijcd,cdk->ijk/dot_general | solution.py:59
  549.8 14.4 %fusion.56 = bf16[32,32,256,32]{2,1,3,0:T(8,128)(2,1)} fusion(bf16[384,256,32]{1,0,2:T(8,128)(2,1)} %get-tuple-element.134, bf16[8,384,32,32]{1,3,2,0:T(8,128)(2,1)} %get-tuple-element.133, s32[]{:T(128)} %get-tuple-element.125), kind=kOutput, calls=%fused_computation.3.clone.1 | convolution fusion | flops 6442450944 | bytes 23855616 | tf_op jit(solution)/shard_map/while/body/eval_jaxpr/sic,sjd->ijcd/dot_general | solution.py:58
  564.2 9.7 %bitcast_dynamic-update-slice_fusion.2 = bf16[8,32,256,128]{3,2,1,0:T(8,128)(2,1)} fusion(bf16[8,32,256,128]{3,2,1,0:T(8,128)(2,1)} %get-tuple-element.126, s32[]{:T(128)} %get-tuple-element.125, bf16[32,32,256,32]{2,1,3,0:T(8,128)(2,1)} %fusion.56, bf16[32,32,128]{2,0,1:T(8,128)(2,1)S(1)} %get-tuple-element.135), kind=kOutput, calls=%fused_computation.6.clone.1 | convolution fusion | flops 2148532224 | bytes 19137024 | tf_op jit(solution)/shard_map/while/body/eval_jaxpr/ijcd,cdk->ijk/dot_general | solution.py:59
  573.9 0.0 reduce-scatter.2.cloned.1.call-update
  574.0 3.9 all-to-all-start.1
  577.9 1.1 convolution_add_fusion
  579.0 0.8 fusion.30
  579.8 0.0 copy-start.4
  579.8 67.7 %all-to-all-done.1 = bf16[256,32,256]{2,1,0:T(8,128)(2,1)} async-done(((bf16[256,32,256]{2,1,0:T(8,128)(2,1)}), bf16[256,32,256]{2,1,0:T(8,128)(2,1)}, u32[]{:S(2)}, u32[]{:S(2)}) %all-to-all-start.1) | async-done | bytes 4194336 | tf_op jit(solution)/shard_map/all_to_all | solution.py:78
  647.5 4.8 copy.88
  652.4 27.1 %convert_bitcast_fusion = bf16[32,256,32,32]{2,3,0,1:T(8,128)(2,1)} fusion(bf16[256,256,32]{0,2,1:T(8,128)(2,1)} %all-gather.2.cloned.1.call-done, bf16[256,32,64]{0,2,1:T(8,128)(2,1)S(1)} %copy-done.4), kind=kOutput, calls=%fused_computation.11 | convolution fusion | flops 4303355904 | bytes 21495808 | tf_op jit(solution)/shard_map/sic,sjd->ijcd/dot_general | solution.py:40
  679.5 84.7 %copy.87 = bf16[32,256,32,32]{1,3,2,0:T(8,128)(2,1)} copy(bf16[32,256,32,32]{2,3,0,1:T(8,128)(2,1)} %convert_bitcast_fusion) | data formatting | bytes 33554432 | tf_op jit(solution)/shard_map/convert_element_type | solution.py:40
  764.1 18.0 %copy.89 = bf16[384,256,64]{1,2,0:T(8,128)(2,1)} copy(bf16[384,256,64]{0,2,1:T(8,128)(2,1)} %bitcast.93) | data formatting | bytes 25165824
  782.1 12.4 %fusion.23 = f32[32,256,128]{2,1,0:T(8,128)} fusion(f32[32,256,128]{2,1,0:T(8,128)} %param.27, bf16[32,256,128]{2,1,0:T(8,128)(2,1)} %reduce-scatter.2.cloned.1.call-done, bf16[32,256,32,32]{1,3,2,0:T(8,128)(2,1)} %copy.87, bf16[32,32,128,1]{2,1,0,3:T(8,128)(2,1)S(1)} %bitcast.90, f32[32,256]{1,0:T(8,128)S(1)} %convolution_add_fusion, ...), kind=kOutput, calls=%fused_computation.29 | convolution fusion | flops 2154823680 | bytes 27591680 | tf_op jit(solution)/shard_map/ijcd,cdk->ijk/dot_general | solution.py:41
  (54 shorter events, 0.2 us)
Async XLA Ops:
  7.2 775.0 %copy-start = (bf16[1024,128]{1,0:T(8,128)(2,1)S(1)}, bf16[1024,128]{1,0:T(8,128)(2,1)}, u32[]{:S(2)}) copy-start(bf16[1024,128]{1,0:T(8,128)(2,1)} %param.42) | copy-start | bytes 786436
  64.8 4.4 copy-start.5
  64.9 4.6 copy-start.13
  64.9 4.6 copy-start.14
  64.9 4.6 copy-start.15
  64.9 4.6 copy-start.16
  64.9 161.2 %all-to-all-start = ((bf16[8,2,393216]{2,1,0:T(2,128)(2,1)}), bf16[8,2,393216]{2,1,0:T(2,128)(2,1)}, u32[]{:S(2)}, u32[]{:S(2)}) async-start(bf16[8,2,393216]{2,1,0:T(2,128)(2,1)} %reshape.113), calls=%async_computation | async-start | bytes 25165824 | tf_op jit(solution)/shard_map/all_to_all | solution.py:75
  69.2 583.2 %all-gather.2.cloned.1.call-start = ((), (), s32[]{:S(2)}) async-start(), calls=%async_computation.4 | async-start | bytes 4718592 | tf_op jit(solution)/shard_map/all_gather | solution.py:39
  69.4 10.9 %copy-start.6 = (s32[256,32]{0,1:T(8,128)}, s32[256,32]{0,1:T(8,128)S(1)}, u32[]{:S(2)}) copy-start(s32[256,32]{0,1:T(8,128)S(1)} %copy.96) | copy-start | bytes 98308
  69.4 7.7 copy-start.1
  69.6 10.7 %copy-start.11 = (bf16[256,32]{0,1:T(8,128)(2,1)S(1)}, bf16[256,32]{0,1:T(8,128)(2,1)}, u32[]{:S(2)}) copy-start(bf16[256,32]{0,1:T(8,128)(2,1)} %param.40) | copy-start | bytes 49156
  69.6 10.7 %copy-start.12 = (bf16[256,32]{0,1:T(8,128)(2,1)S(1)}, bf16[256,32]{0,1:T(8,128)(2,1)}, u32[]{:S(2)}) copy-start(bf16[256,32]{0,1:T(8,128)(2,1)} %param.38) | copy-start | bytes 49156
  77.1 7.7 copy-start.17
  77.1 7.7 copy-start.18
  77.1 7.7 copy-start.8
  77.2 7.8 copy-start.19
  77.2 7.8 copy-start.20
  82.9 1.0 copy-start.3
  84.7 697.4 %reduce-scatter.2.cloned.1.call-start = ((), (), s32[]{:S(2)}) async-start(), calls=%async_computation.3 | async-start | bytes 18874368 | tf_op jit(solution)/shard_map/reduce_scatter | solution.py:62
  332.1 18.2 %copy-start.9 = (bf16[64,32]{0,1:T(8,128)(2,1)S(1)}, bf16[64,32]{0,1:T(8,128)(2,1)}, u32[]{:S(2)}) copy-start(bf16[64,32]{0,1:T(8,128)(2,1)} %param.32) | copy-start | bytes 12292
  332.1 18.2 %copy-start.10 = (bf16[64,32]{0,1:T(8,128)(2,1)S(1)}, bf16[64,32]{0,1:T(8,128)(2,1)}, u32[]{:S(2)}) copy-start(bf16[64,32]{0,1:T(8,128)(2,1)} %param.30) | copy-start | bytes 12292
  573.9 3.9 copy-start.21
  573.9 3.9 copy-start.22
  574.0 3.9 copy-start.7
  574.0 5.0 copy-start.2
  574.0 73.5 %all-to-all-start.1 = ((bf16[256,32,256]{2,1,0:T(8,128)(2,1)}), bf16[256,32,256]{2,1,0:T(8,128)(2,1)}, u32[]{:S(2)}, u32[]{:S(2)}) async-start(bf16[256,32,256]{2,1,0:T(8,128)(2,1)} %param.25), calls=%async_computation.2 | async-start | bytes 8388608 | tf_op jit(solution)/shard_map/all_to_all | solution.py:78
  579.8 72.5 %copy-start.4 = (bf16[256,32,64]{0,2,1:T(8,128)(2,1)S(1)}, bf16[256,32,64]{0,2,1:T(8,128)(2,1)}, u32[]{:S(2)}) copy-start(bf16[256,32,64]{0,2,1:T(8,128)(2,1)} %copy-done.3) | copy-start | bytes 3145732
Sparse Core Ops, SparseCore 0:
  84.8 86.1 all-gather.1
  574.1 126.4 reduce-scatter.1
where the time goes:
time: 815 us; the launch traced here: 802 us
  local copies, waits for them, and re-layouts  287 us (35%)
  matrix products  244 us (30%)
  waiting for transfers between devices  208 us (26%)
  other arithmetic  39.8 us (5%)
  between operations  14.9 us (2%)
  starting transfers between devices  8.25 us (1%)
    all_to_all x1, waiting for transfers between devices, local_program(): extra_relaid = lax.all_to_all(extra_block, 'dap', 0, 1, tiled=True)  140 us
    dot_general x8, matrix products, block_partial(): jnp.einsum('sic,sjd->ijcd', left_block, right_proj, preferred_element_typ...  115 us
    unnamed x51, local copies, waits for them, and re-layouts  99.5 us
    convert_element_type x1, local copies, waits for them, and re-layouts, gathered_term(): jnp.einsum('sic,sjd->ijcd', left_proj, right_all, preferred_element_type=...  84.7 us
    dot_general x8, matrix products, block_partial(): jnp.einsum('ijcd,cdk->ijk', outer_prod, w_grid, preferred_element_type=jn...  77.9 us
    all_to_all x1, waiting for transfers between devices, local_program(): main_relaid = lax.all_to_all(main_block, 'dap', 0, 1, tiled=True)  67.7 us
    all_to_all x2, local copies, waits for them, and re-layouts, local_program(): extra_relaid = lax.all_to_all(extra_block, 'dap', 0, 1, tiled=True)  55.2 us
    dot_general x1, matrix products, gathered_term(): jnp.einsum('sic,sjd->ijcd', left_proj, right_all, preferred_element_type=...  27.1 us
  transfers between devices with their start and end apart: 4, of which 2 were waited for; matrix products, arithmetic and copies ran while one was open for 62% of the time, Pallas kernels for 0%

commit v1 on v0

v1 whole, which is shorter than its diff:
```python
import functools

import jax
import jax.numpy as jnp
from jax import lax
from jax.experimental import pallas as pl
from jax.experimental.pallas import tpu as pltpu
from jax.sharding import PartitionSpec as P

LN_EPS = 1e-5
NORM_EPS = 1e-3
BF = jnp.bfloat16
F32 = jnp.float32
GROUP = 16
QSTEP = 4
RSTEP = 8


def partner(me, k):
    core, cx, cy = me % 2, (me // 2) % 2, me // 4
    k0, k1, k2 = k % 2, (k // 2) % 2, k // 4
    return (core + k0) % 2 + 2 * ((cx + k1) % 2) + 4 * ((cy + k2) % 2)


def nt_dot(lhs, rhs):
    return lax.dot_general(lhs, rhs, (((1,), (1,)), ((), ())), preferred_element_type=F32)


def opm_kernel(
    xe, xm, mask_e, mask_m, pair,
    gam_e, bet_e, w_blk, bias_b, bias_a, wo_e, bo_e, cnt_e,
    gam_m, bet_m, w_m, bias_m, wo_m, bo_m, cnt_m,
    pair_out, e_out, m_out, rs_recv,
    a_all, b_all, a_send, xb, y_s, mask_i, mask_et, mask_mt, mask_mo, am, bm, rt,
    e_ssem, e_rsem, m_ssem, m_rsem, xa_ssem, xa_rsem, xb_ssem, xb_rsem,
    g_ssem, g_rsem, f_ssem, f_rsem, rs_ssem, rs_rsem, lsem,
):
    me = lax.axis_index('dap')
    core = me % 2
    chip = me // 2
    sib = partner(me, 1)
    seq = e_out.shape[2]
    mseq = m_out.shape[0]
    rows = xe.shape[0]
    res = e_out.shape[0]

    def dev(d):
        return {'dap': d}

    def lane(h):
        return pl.ds(pl.multiple_of(h * seq, 128), seq)

    def rblk(d, n=rows):
        return pl.ds(pl.multiple_of(d * n, n), n)

    barrier = pltpu.get_barrier_semaphore()
    for k in range(1, 8):
        pl.semaphore_signal(barrier, inc=1, device_id=dev(partner(me, k)), device_id_type=pl.DeviceIdType.MESH)
    pl.semaphore_wait(barrier, 7)

    def remote(src, dst, ssem, rsem, target):
        return pltpu.make_async_remote_copy(
            src_ref=src, dst_ref=dst, send_sem=ssem, recv_sem=rsem,
            device_id=dev(target), device_id_type=pl.DeviceIdType.MESH)

    def e_copy(k):
        to = partner(me, k)
        return remote(xe.at[:, :, lane(to)], e_out.at[rblk(me)], e_ssem.at[k], e_rsem.at[k], to)

    for k in (1, 2, 4, 3, 5, 6, 7):
        e_copy(k).start()

    def m_copy(k):
        to = partner(me, k)
        return remote(xm.at[rblk(to, mseq)], m_out.at[:, rblk(me), :], m_ssem.at[k], m_rsem.at[k], to)

    cp = pltpu.make_async_copy(mask_e.at[rblk(me, seq)], mask_i, lsem.at[0])
    cp.start()
    mask_mt[...] = mask_m[...].astype(F32).T
    mask_mo[...] = mask_mt[rblk(me), :].reshape(rows, 1, mask_m.shape[0])
    cp.wait()
    mask_et[...] = mask_i[...].astype(F32).T

    def main_proj(xc, xf, bf):
        cp = pltpu.make_async_copy(xm.at[rblk(me, mseq)], xc.at[pl.ds(0, mseq)], lsem.at[1])
        cp.start()
        cp.wait()
        cp = pltpu.make_async_copy(xc.at[pl.ds(0, mseq)], m_out.at[:, rblk(me), :], lsem.at[1])
        cp.start()
        cp.wait()
        step = xc.shape[0]
        for part in range(xm.shape[0] // step):
            cp = pltpu.make_async_copy(xm.at[pl.ds(part * step, step)], xc, lsem.at[2])
            cp.start()
            cp.wait()

            def widen(i, _):
                s = pl.ds(pl.multiple_of(i * 8, 8), 8)
                xf[s] = xc[s].astype(F32)
                return 0
            lax.fori_loop(0, step // 8, widen, 0)

            def one(r, _):
                x = xf[:, r, :]
                mean = jnp.mean(x, axis=1, keepdims=True)
                cen = x - mean
                var = jnp.mean(cen * cen, axis=1, keepdims=True)
                y = (cen * lax.rsqrt(var + LN_EPS) * gam_m[...] + bet_m[...]).astype(BF)
                proj = nt_dot(w_m[...], y) + bias_m[...]
                proj = proj * mask_mo[r, :, pl.ds(part * step, step)]
                am[pl.ds(pl.multiple_of(r * 32, 32), 32), pl.ds(part * step, step)] = proj[:32].astype(BF)
                bf[:, r, :] = proj[32:]
                return 0
            lax.fori_loop(0, rows, one, 0)
            bm[:, rblk(me), pl.ds(part * step, step)] = bf[...].astype(BF)

    pl.run_scoped(
        main_proj, pltpu.VMEM((128, rows, xm.shape[2]), BF), pltpu.VMEM((128, rows, xm.shape[2]), F32),
        pltpu.VMEM((32, rows, 128), F32))

    def xb_copy(src):
        ref = b_all.at[:, rblk(src), lane(core)]
        return remote(ref, ref, xb_ssem.at[src], xb_rsem.at[src], sib)

    def xb_wait(src):
        ref = b_all.at[:, rblk(src), lane(1 - core)]
        return remote(ref, ref, xb_ssem.at[src], xb_rsem.at[src], sib)

    def xa_copy(c):
        return remote(a_send.at[rblk(c, rows * 32)], a_all.at[rblk(c, rows * 32), lane(core)],
                      xa_ssem.at[c], xa_rsem.at[c], sib)

    def xa_wait(c):
        return remote(a_send.at[rblk(c, rows * 32)], a_all.at[rblk(c, rows * 32), lane(1 - core)],
                      xa_ssem.at[c], xa_rsem.at[c], sib)

    def block(k, _):
        src = partner(me, k)
        own_half = (src % 2 + core) % 2

        @pl.when(k == 0)
        def _():
            cp = pltpu.make_async_copy(xe.at[:, :, lane(me)], xb, lsem.at[0])
            cp.start()
            cp.wait()
            cp = pltpu.make_async_copy(xb, e_out.at[rblk(me)], lsem.at[0])
            cp.start()
            cp.wait()

        @pl.when(k > 0)
        def _():
            remote(xe.at[:, :, lane(src)], e_out.at[rblk(src)], e_ssem.at[k], e_rsem.at[k], src).wait_recv()
            cp = pltpu.make_async_copy(e_out.at[rblk(src)], xb, lsem.at[0])
            cp.start()
            cp.wait()

        def half(hh, _):
            def norm(i, _):
                for u in range(2):
                    r = i * 2 + u
                    x = xb[hh * GROUP + r].astype(F32)
                    mean = jnp.mean(x, axis=0, keepdims=True)
                    cen = x - mean
                    var = jnp.mean(cen * cen, axis=0, keepdims=True)
                    y = cen * lax.rsqrt(var + LN_EPS) * gam_e[...] + bet_e[...]
                    y_s[pl.ds(pl.multiple_of(r * 64, 64), 64), :] = y.astype(BF)
                return 0
            lax.fori_loop(0, GROUP // 2, norm, 0)
            r0 = pl.multiple_of(src * rows + hh * GROUP, GROUP)
            m16 = mask_et[pl.ds(r0, GROUP), :]
            right = jnp.dot(w_blk[:512], y_s[...], preferred_element_type=F32) + bias_b[...]
            right = right.reshape(32, GROUP, seq) * m16[None]
            b_all[:, pl.ds(r0, GROUP), lane(core)] = right.astype(BF)
            left = jnp.dot(w_blk[512:], y_s[...], preferred_element_type=F32)
            left = jnp.concatenate(
                [(left[r * 32:r * 32 + 32] + bias_a[...]) * m16[r:r + 1] for r in range(GROUP)], axis=0).astype(BF)
            at = pl.ds(pl.multiple_of(((src // 2) * rows + hh * GROUP) * 32, GROUP * 32), GROUP * 32)

            @pl.when(own_half == 0)
            def _():
                a_all[at, lane(core)] = left

            @pl.when(own_half == 1)
            def _():
                a_send[at, :] = left
            return 0
        lax.fori_loop(0, rows // GROUP, half, 0)
        xb_copy(src).start()

        @pl.when(own_half == 1)
        def _():
            xa_copy(src // 2).start()
        return 0
    lax.fori_loop(0, 8, block, 0)

    for k in range(1, 8):
        e_copy(k).wait_send()

    def g_copy(i):
        ref = bm.at[:, rblk(me), :]
        return remote(ref, ref, g_ssem.at[i], g_rsem.at[i], partner(me, (1, 2, 4, 6)[i]))

    def g_wait(i):
        to = partner(me, (1, 2, 4, 6)[i])
        ref = bm.at[:, rblk(to), :]
        return remote(ref, ref, g_ssem.at[i], g_rsem.at[i], to)

    def f_copy(i):
        ref = bm.at[:, rblk(partner(me, (2, 4, 6)[i])), :]
        return remote(ref, ref, f_ssem.at[i], f_rsem.at[i], sib)

    def f_wait(i):
        ref = bm.at[:, rblk(partner(me, (3, 5, 7)[i])), :]
        return remote(ref, ref, f_ssem.at[i], f_rsem.at[i], sib)

    for i in range(4):
        g_copy(i).start()
    for k in (1, 2, 4, 3, 5, 6, 7):
        m_copy(k).start()

    def xwait(s, _):
        xb_wait(s).wait_recv()
        return 0
    lax.fori_loop(0, 8, xwait, 0)

    def xwait_a(c, _):
        xa_wait(c).wait_recv()
        return 0
    lax.fori_loop(0, 4, xwait_a, 0)

    def rs_copy(t, ib):
        to = partner(me, 6 - 2 * t)
        at = pl.ds(pl.multiple_of(ib * GROUP, GROUP), GROUP)
        return remote(rt.at[t, at], rs_recv.at[t, at], rs_ssem.at[t * 2 + ib], rs_rsem.at[t * 2 + ib], to)

    def contract(o_s, tm):
        def outer(left, right_of):
            def qstep(qq, _):
                for u in range(QSTEP):
                    q = qq * QSTEP + u
                    o = nt_dot(left(), right_of(q))
                    o_s[:, pl.ds(pl.multiple_of(q * 32, 32), 32), :] = o.astype(BF).reshape(GROUP, 32, res)
                return 0
            lax.fori_loop(0, 32 // QSTEP, qstep, 0)

        def eblk(n, _):
            t, ib = n // 2, n % 2
            c = partner(me, 6 - 2 * t) // 2
            at = pl.ds(pl.multiple_of((c * rows + ib * GROUP) * 32, GROUP * 32), GROUP * 32)
            outer(lambda: a_all[at, :], lambda q: b_all[q])

            def rstep(ii, _):
                for u in range(RSTEP):
                    i = ii * RSTEP + u
                    rt[t, ib * GROUP + i] = jnp.dot(wo_e[...], o_s[i], preferred_element_type=F32).astype(BF)
                return 0
            lax.fori_loop(0, GROUP // RSTEP, rstep, 0)

            @pl.when(t < 3)
            def _():
                rs_copy(t, ib).start()
            return 0
        lax.fori_loop(0, 8, eblk, 0)

        for i in range(1, 4):
            g_wait(i).wait_recv()
            f_copy(i - 1).start()
        g_wait(0).wait_recv()
        for i in range(3):
            f_wait(i).wait_recv()

        def mblk(ib, _):
            at = pl.ds(pl.multiple_of(ib * GROUP * 32, GROUP * 32), GROUP * 32)
            outer(lambda: am[at, :], lambda q: bm[q])

            def rstep(ii, _):
                for u in range(RSTEP):
                    i = ii * RSTEP + u
                    row = ib * GROUP + i
                    r = jnp.dot(wo_m[...], o_s[i], preferred_element_type=F32)
                    tm[row] = (r + bo_m[...]) / (NORM_EPS + cnt_m[row])
                return 0
            lax.fori_loop(0, GROUP // RSTEP, rstep, 0)
            return 0
        lax.fori_loop(0, rows // GROUP, mblk, 0)

        def final(zb, rb):
            def z_copy(j):
                return pltpu.make_async_copy(pair.at[pl.ds(j * 8, 8)], zb.at[j % 2], lsem.at[3 + j % 2])

            def o_copy(j):
                return pltpu.make_async_copy(zb.at[j % 2], pair_out.at[pl.ds(j * 8, 8)], lsem.at[5 + j % 2])

            def r_copy(j):
                return pltpu.make_async_copy(rs_recv.at[:, pl.ds(j * 8, 8)], rb, lsem.at[7])

            z_copy(0).start()
            for j in range(rows // 8):
                if j % 2 == 0:
                    for t in range(3):
                        rs_copy(t, j // 2).wait_recv()
                r_copy(j).start()
                if j >= 1:
                    o_copy(j - 1).wait()
                if j + 1 < rows // 8:
                    z_copy(j + 1).start()
                z_copy(j).wait()
                r_copy(j).wait()

                def row(i, _):
                    n = j * 8 + i
                    tot = rt[3, n].astype(F32) + rb[0, i].astype(F32) + rb[1, i].astype(F32) + rb[2, i].astype(F32)
                    te = (tot + bo_e[...]) / (NORM_EPS + cnt_e[n])
                    zb[j % 2, i] = (zb[j % 2, i] + te.T) + tm[n].T
                    return 0
                lax.fori_loop(0, 8, row, 0)
                o_copy(j).start()
            o_copy(rows // 8 - 1).wait()

        pl.run_scoped(final, pltpu.VMEM((2, 8, res, 128), F32), pltpu.VMEM((3, 8, 128, res), BF))

    pl.run_scoped(contract, pltpu.VMEM((GROUP, 1024, res), BF), pltpu.VMEM((rows, 128, res), F32))

    for k in range(1, 8):
        m_copy(k).wait_send()
        to = partner(me, k)
        remote(xm.at[rblk(me, mseq)], m_out.at[:, rblk(to), :], m_ssem.at[k], m_rsem.at[k], to).wait_recv()

    def drain(s, _):
        xb_copy(s).wait_send()
        return 0
    lax.fori_loop(0, 8, drain, 0)

    def drain_a(c, _):
        xa_copy(c).wait_send()
        return 0
    lax.fori_loop(0, 4, drain_a, 0)
    for i in range(4):
        g_copy(i).wait_send()
    for i in range(3):
        f_copy(i).wait_send()
        for ib in range(2):
            rs_copy(i, ib).wait_send()


def pair_counts(mask_rows, mask_full):
    return jnp.einsum('si,sj->ij', mask_rows.astype(BF), mask_full.astype(BF), preferred_element_type=F32)


def column(v):
    return v.astype(F32)[:, None]


def solution(mesh):
    msa_spec = P('data', 'dap', None)
    mask_spec = P('data', None)
    row_spec = P(('data', 'dap'), None, None)

    def local_program(extra_block, extra_mask, main_block, main_mask, pair_rows,
                      e_gam, e_bet, e_wl, e_bl, e_wr, e_br, e_wo, e_bo,
                      m_gam, m_bet, m_wl, m_bl, m_wr, m_br, m_wo, m_bo):
        seqs, rows, ce = extra_block.shape
        mseqs, _, cm = main_block.shape
        res = extra_mask.shape[1]
        hid = e_wl.shape[1]
        nk = e_wo.shape[1]
        me = lax.axis_index('dap')
        seq = seqs // 8

        def counts(mask):
            return pair_counts(lax.dynamic_slice_in_dim(mask, me * rows, rows, axis=1), mask)[:, None, :]

        eye = jnp.eye(GROUP, dtype=BF)
        w_b = (e_wr.T[:, None, None, :] * eye[None, :, :, None]).reshape(hid * GROUP, GROUP * ce)
        w_a = (e_wl.T[None, :, None, :] * eye[:, None, :, None]).reshape(hid * GROUP, GROUP * ce)
        w_blk = jnp.concatenate([w_b, w_a], axis=0)
        bias_b = jnp.repeat(e_br.astype(F32), GROUP)[:, None]

        def w_out_t(w):
            return w.reshape(hid, hid, nk).transpose(2, 1, 0).reshape(nk, hid * hid)

        args = (
            jnp.transpose(extra_block, (1, 2, 0)), main_block, extra_mask, main_mask, pair_rows,
            column(e_gam), column(e_bet), w_blk, bias_b, column(e_bl), w_out_t(e_wo), column(e_bo), counts(extra_mask),
            m_gam.astype(F32)[None], m_bet.astype(F32)[None], jnp.concatenate([m_wl.T, m_wr.T], axis=0),
            column(jnp.concatenate([m_bl, m_br])), w_out_t(m_wo), column(m_bo), counts(main_mask))
        any_spec = pl.BlockSpec(memory_space=pl.ANY)
        vmem = pl.BlockSpec(memory_space=pltpu.VMEM)
        dma = pltpu.SemaphoreType.DMA
        pair_out, e_recv, m_recv, _ = pl.pallas_call(
            opm_kernel,
            out_shape=(
                jax.ShapeDtypeStruct((rows, res, nk), F32),
                jax.ShapeDtypeStruct((res, ce, seq), BF),
                jax.ShapeDtypeStruct((mseqs // 8, res, cm), BF),
                jax.ShapeDtypeStruct((3, rows, nk, res), BF)),
            in_specs=[any_spec, any_spec, any_spec, vmem, any_spec] + [vmem] * 15,
            out_specs=(any_spec,) * 4,
            scratch_shapes=[
                pltpu.VMEM((4 * rows * hid, 2 * seq), BF),
                pltpu.VMEM((hid, res, 2 * seq), BF),
                pltpu.VMEM((4 * rows * hid, seq), BF),
                pltpu.VMEM((rows, ce, seq), BF),
                pltpu.VMEM((GROUP * ce, seq), BF),
                pltpu.VMEM((seq, res), jnp.int32),
                pltpu.VMEM((res, seq), F32),
                pltpu.VMEM((res, mseqs), F32),
                pltpu.VMEM((rows, 1, mseqs), F32),
                pltpu.VMEM((rows * hid, mseqs), BF),
                pltpu.VMEM((hid, res, mseqs), BF),
                pltpu.VMEM((4, rows, nk, res), BF),
                dma((8,)), dma((8,)), dma((8,)), dma((8,)), dma((4,)), dma((4,)), dma((8,)), dma((8,)),
                dma((4,)), dma((4,)), dma((3,)), dma((3,)), dma((6,)), dma((6,)), dma((8,))],
            compiler_params=pltpu.CompilerParams(
                collective_id=0, has_side_effects=True, vmem_limit_bytes=67043328),
            name='opm',
        )(*args)
        return pair_out, jnp.transpose(e_recv, (2, 0, 1)), m_recv

    in_specs = (msa_spec, mask_spec, msa_spec, mask_spec, row_spec) + (P(),) * 16
    return jax.shard_map(local_program, mesh=mesh, in_specs=in_specs, out_specs=(row_spec,) * 3, check_vma=False)
```

time: 815 us -> 371 us (0.46); the launches traced: 802 us -> 369 us
  Pallas kernels: 0 us -> 317 us
  local copies, waits for them, and re-layouts: 287 us -> 37.7 us
  matrix products: 244 us -> 3.42 us
  waiting for transfers between devices: 208 us -> 0 us
  other arithmetic: 39.8 us -> 11.1 us
  between operations: 14.9 us -> 0.73 us
  starting transfers between devices: 8.25 us -> 0 us
    pallas_call x0 -> x1, Pallas kernels: none -> 317 us  [local_program(): pl.pallas_call(opm_kernel, out_shape=(jax.ShapeDtypeStruct((rows, res, nk...]
    dot_general x22 -> x2, matrix products: 244 us -> 3.42 us  [pair_counts(): jnp.einsum('si,sj->ij', mask_rows.astype(BF), mask_full.astype(BF), prefe...]
    all_to_all x2 -> x0, waiting for transfers between devices: 208 us -> none  [the longest x1 140 us: local_program(): extra_relaid = lax.all_to_all(extra_block, 'dap', 0, 1, tiled=True)]
    convert_element_type x2 -> x1, local copies, waits for them, and re-layouts: 103 us -> 0.7 us  [column(): return v.astype(F32)[:, None]]
    unnamed x51 -> x15, local copies, waits for them, and re-layouts: 99.5 us -> 24.8 us
    all_to_all x3 -> x0, local copies, waits for them, and re-layouts: 60 us -> none  [the longest x2 55.2 us: local_program(): extra_relaid = lax.all_to_all(extra_block, 'dap', 0, 1, tiled=True)]
    reduce_sum x4 -> x0, other arithmetic: 22.5 us -> none  [the longest x2 12.5 us: layer_norm(): row_var = jnp.mean(centered * centered, axis=-1, keepdims=True)]
    convert_element_type x12 -> x2, other arithmetic: 17.2 us -> 0.75 us  [the longest x1 0.75 us: column(): return v.astype(F32)[:, None]]
  transfers between devices with their start and end apart: 4 -> 0, of which waited for: 2 -> 0; matrix products, arithmetic and copies ran while one was open for 62% -> 0% of each run, Pallas kernels for 0% -> 0%
where the time goes in v1:
time: 371 us; the launch traced here: 369 us
  Pallas kernels  317 us (85%)
  local copies, waits for them, and re-layouts  37.7 us (10%)
  other arithmetic  11.1 us (3%)
    pallas_call x1, Pallas kernels, local_program(): pl.pallas_call(opm_kernel, out_shape=(jax.ShapeDtypeStruct((rows, res, nk...  317 us
    unnamed x15, local copies, waits for them, and re-layouts  24.8 us

profile of v1, /device:TPU:0, one launch (start us, length us, event | category | flops | bytes accessed | tf_op | source)
XLA Modules:
  0.0 369.5 jit_solution(2084020430193630535)
XLA Ops:
  0.6 0.0 copy-start.1
  0.6 0.0 copy-start.3
  0.7 0.0 copy-start.2
  0.7 0.7 bitcast_convert_fusion.4
  1.4 0.7 bitcast_convert_fusion.3
  2.1 0.7 bitcast_convert_fusion.2
  2.7 0.7 bitcast_convert_fusion.1
  3.4 0.7 maximum_convert_fusion
  4.1 0.7 bitcast_convert_fusion
  4.8 1.2 broadcast_in_dim.70
  6.0 1.2 broadcast_in_dim.71
  7.3 0.7 copy.75.bias_a
  7.9 0.0 copy-start.4
  7.9 0.7 broadcast_in_dim.53
  8.7 0.7 copy.78.bias_m
  9.4 0.7 copy.73.bet_e
  10.1 0.7 copy.72.gam_e
  10.8 1.4 pad_maximum_fusion.1.w_m
  12.2 3.2 fusion
  15.3 0.6 broadcast_in_dim.58.cnt_e
  16.0 0.0 copy-done.1
  16.0 0.2 fusion.2
  16.2 0.6 broadcast_in_dim.65.cnt_m
  16.9 0.7 copy.80.bo_m
  17.6 0.7 copy.77.bo_e
  18.3 0.9 broadcast_in_dim_reshape.4.bias_b
  19.2 0.0 copy-done.2
  19.2 0.1 copy.70
  19.3 0.9 copy.76.wo_e
  20.2 0.0 copy-done.3
  20.2 0.0 copy-start.5
  20.2 0.1 copy.71
  20.3 0.9 copy.79.wo_m
  21.1 0.0 copy-done.4
  21.1 0.2 broadcast_multiply_fusion
  21.4 1.5 mul.45
  22.8 0.0 copy-done.5
  22.9 0.2 broadcast_multiply_fusion.1
  23.1 2.3 mul.41
  25.4 2.7 pad_maximum_fusion.w_blk
  28.1 316.6 %opm.1 = (f32[32,256,128]{2,1,0:T(8,128)}, bf16[256,64,384]{2,1,0:T(8,128)(2,1)}, bf16[32,256,256]{2,1,0:T(8,128)(2,1)}, bf16[3,32,128,256]{3,2,1,0:T(8,128)(2,1)}) custom-call(bf16[32,64,3072]{2,1,0:T(8,128)(2,1)} %bitcast.37, bf16[256,32,256]{2,1,0:T(8,128)(2,1)} %xm.1, s32[3072,256]{1,0:T(8,128)} %mask_e.1, s32[256,256]{1,0:T(8,128)} %mask_m.1, ...), custom_call_target="tpu_custom_call" | custom-call | tf_op jit(solution)/shard_map/opm/pallas_call | solution.py:390
  344.7 18.0 %copy.81 = bf16[384,256,64]{1,2,0:T(8,128)(2,1)} copy(bf16[384,256,64]{0,2,1:T(8,128)(2,1)} %bitcast.38) | data formatting | bytes 25165824
  362.7 0.0 copy-start
  362.7 4.8 %copy.84 = f32[32,256,128]{2,1,0:T(8,128)} copy(f32[32,256,128]{2,1,0:T(8,128)} %get-tuple-element.27) | data formatting | bytes 8388608
  367.5 0.0 copy-done
  367.5 2.0 copy.85
  (1 shorter events, 0.0 us)
Async XLA Ops:
  0.6 15.3 %copy-start.1 = (s32[256,256]{1,0:T(8,128)S(1)}, s32[256,256]{1,0:T(8,128)}, u32[]{:S(2)}) copy-start(s32[256,256]{1,0:T(8,128)} %mask_m.1) | copy-start | bytes 786436
  0.6 19.5 %copy-start.3 = (bf16[1024,128]{1,0:T(8,128)(2,1)S(1)}, bf16[1024,128]{1,0:T(8,128)(2,1)}, u32[]{:S(2)}) copy-start(bf16[1024,128]{1,0:T(8,128)(2,1)} %param.40) | copy-start | bytes 786436
  0.7 18.5 %copy-start.2 = (bf16[1024,128]{1,0:T(8,128)(2,1)S(1)}, bf16[1024,128]{1,0:T(8,128)(2,1)}, u32[]{:S(2)}) copy-start(bf16[1024,128]{1,0:T(8,128)(2,1)} %param.32) | copy-start | bytes 786436
  7.9 13.2 %copy-start.4 = (bf16[64,32]{0,1:T(8,128)(2,1)S(1)}, bf16[64,32]{0,1:T(8,128)(2,1)}, u32[]{:S(2)}) copy-start(bf16[64,32]{0,1:T(8,128)(2,1)} %param.28) | copy-start | bytes 12292
  20.2 2.7 copy-start.5
  362.7 4.8 %copy-start = (bf16[32,256,256]{2,1,0:T(8,128)(2,1)S(1)}, bf16[32,256,256]{2,1,0:T(8,128)(2,1)}, u32[]{:S(2)}) copy-start(bf16[32,256,256]{2,1,0:T(8,128)(2,1)} %get-tuple-element.29) | copy-start | bytes 12582916

commit v2 on v1

--- a/solution.py
+++ b/solution.py
@@ -26,12 +26,19 @@
     return lax.dot_general(lhs, rhs, (((1,), (1,)), ((), ())), preferred_element_type=F32)
 
 
+def column(row, n, repeat):
+    m = row.shape[1]
+    at = lax.broadcasted_iota(jnp.int32, (n, m), 0) // repeat
+    return jnp.sum(jnp.where(at == lax.broadcasted_iota(jnp.int32, (n, m), 1), row, 0.0), axis=1, keepdims=True)
+
+
 def opm_kernel(
     xe, xm, mask_e, mask_m, pair,
-    gam_e, bet_e, w_blk, bias_b, bias_a, wo_e, bo_e, cnt_e,
-    gam_m, bet_m, w_m, bias_m, wo_m, bo_m, cnt_m,
+    e_gam, e_bet, e_wl, e_bl, e_wr, e_br, e_wo, e_bo,
+    m_gam, m_bet, m_wl, m_bl, m_wr, m_br, m_wo, m_bo,
     pair_out, e_out, m_out, rs_recv,
-    a_all, b_all, a_send, xb, y_s, mask_i, mask_et, mask_mt, mask_mo, am, bm, rt,
+    a_all, b_all, a_send, xb, y_s, mask_i, mask_et, mask_mo, am, bm, rt, rs_mid,
+    w_blk, w_m, wo_e, wo_m, gam_e, bet_e, bias_b, bias_a, bo_e, bias_m, bo_m, cnt_e, cnt_m,
     e_ssem, e_rsem, m_ssem, m_rsem, xa_ssem, xa_rsem, xb_ssem, xb_rsem,
     g_ssem, g_rsem, f_ssem, f_rsem, rs_ssem, rs_rsem, lsem,
 ):
@@ -74,12 +81,68 @@
         to = partner(me, k)
         return remote(xm.at[rblk(to, mseq)], m_out.at[:, rblk(me), :], m_ssem.at[k], m_rsem.at[k], to)
 
-    cp = pltpu.make_async_copy(mask_e.at[rblk(me, seq)], mask_i, lsem.at[0])
-    cp.start()
-    mask_mt[...] = mask_m[...].astype(F32).T
-    mask_mo[...] = mask_mt[rblk(me), :].reshape(rows, 1, mask_m.shape[0])
-    cp.wait()
-    mask_et[...] = mask_i[...].astype(F32).T
+    def row_of(ref):
+        v = ref[...].astype(F32)
+        return v.reshape(1, v.shape[0])
+
+    def weights(wf, wp):
+        gam_e[...] = column(row_of(e_gam), 64, 1)
+        bet_e[...] = column(row_of(e_bet), 64, 1)
+        bias_b[...] = column(row_of(e_br), 32 * GROUP, GROUP)
+        bias_a[...] = column(row_of(e_bl), 32, 1)
+        bo_e[...] = column(row_of(e_bo), 128, 1)
+        bo_m[...] = column(row_of(m_bo), 128, 1)
+        bias_m[:32] = column(row_of(m_bl), 32, 1)
+        bias_m[32:] = column(row_of(m_br), 32, 1)
+        w_m[:32] = m_wl[...]
+        w_m[32:] = m_wr[...]
+        at_col = lax.broadcasted_iota(jnp.int32, (32 * GROUP, 64 * GROUP), 1) // 64
+        at_row = lax.broadcasted_iota(jnp.int32, (32 * GROUP, 64 * GROUP), 0)
+
+        def wide(ref):
+            w = ref[...].astype(F32)
+            return jnp.concatenate([jnp.concatenate([w, w], axis=1)] * (GROUP // 2), axis=1)
+
+        rep = jnp.broadcast_to(wide(e_wr)[:, None, :], (32, GROUP, 64 * GROUP)).reshape(32 * GROUP, 64 * GROUP)
+        w_blk[:32 * GROUP] = jnp.where(at_row % GROUP == at_col, rep, 0.0).astype(BF)
+        rep = jnp.concatenate([wide(e_wl)] * GROUP, axis=0)
+        w_blk[32 * GROUP:] = jnp.where(at_row // 32 == at_col, rep, 0.0).astype(BF)
+        for src, dst in ((e_wo, wo_e), (m_wo, wo_m)):
+            wf[...] = src[...].astype(F32)
+
+            def pick(q, _):
+                wp[pl.ds(pl.multiple_of(q * 32, 32), 32), :] = wf[pl.ds(q, 32, stride=32), :]
+                return 0
+            lax.fori_loop(0, 32, pick, 0)
+            dst[...] = wp[...].T.astype(BF)
+
+    pl.run_scoped(weights, pltpu.VMEM((1024, 128), F32), pltpu.VMEM((1024, 128), F32))
+
+    def masks(mt, acc):
+        mt[:, :mask_m.shape[0]] = mask_m[...].astype(F32).T
+        own = mt[rblk(me), :mask_m.shape[0]]
+        mask_mo[...] = own.reshape(rows, 1, mask_m.shape[0])
+        cnt_m[...] = jnp.dot(own.astype(BF), mask_m[...].astype(F32).astype(BF),
+                             preferred_element_type=F32).reshape(rows, 1, res)
+        acc[...] = jnp.zeros_like(acc)
+
+        def load(d):
+            cp = pltpu.make_async_copy(mask_e.at[rblk(d, seq)], mask_i, lsem.at[0])
+            cp.start()
+            cp.wait()
+
+        def count(d, _):
+            load(d)
+            m = mask_i[...].astype(F32)
+            mt[...] = m.T
+            acc[...] += jnp.dot(mt[rblk(me), :].astype(BF), m.astype(BF), preferred_element_type=F32)
+            return 0
+        lax.fori_loop(0, 8, count, 0)
+        cnt_e[...] = acc[...].reshape(rows, 1, res)
+        load(me)
+        mask_et[...] = mask_i[...].astype(F32).T
+
+    pl.run_scoped(masks, pltpu.VMEM((res, seq), F32), pltpu.VMEM((rows, res), F32))
 
     def main_proj(xc, xf, bf):
         cp = pltpu.make_async_copy(xm.at[rblk(me, mseq)], xc.at[pl.ds(0, mseq)], lsem.at[1])
@@ -89,6 +152,7 @@
         cp.start()
         cp.wait()
         step = xc.shape[0]
+        gam_m, bet_m = row_of(m_gam), row_of(m_bet)
         for part in range(xm.shape[0] // step):
             cp = pltpu.make_async_copy(xm.at[pl.ds(part * step, step)], xc, lsem.at[2])
             cp.start()
@@ -105,7 +169,7 @@
                 mean = jnp.mean(x, axis=1, keepdims=True)
                 cen = x - mean
                 var = jnp.mean(cen * cen, axis=1, keepdims=True)
-                y = (cen * lax.rsqrt(var + LN_EPS) * gam_m[...] + bet_m[...]).astype(BF)
+                y = (cen * lax.rsqrt(var + LN_EPS) * gam_m + bet_m).astype(BF)
                 proj = nt_dot(w_m[...], y) + bias_m[...]
                 proj = proj * mask_mo[r, :, pl.ds(part * step, step)]
                 am[pl.ds(pl.multiple_of(r * 32, 32), 32), pl.ds(part * step, step)] = proj[:32].astype(BF)
@@ -215,8 +279,7 @@
 
     for i in range(4):
         g_copy(i).start()
-    for k in (1, 2, 4, 3, 5, 6, 7):
-        m_copy(k).start()
+    m_copy(1).start()
 
     def xwait(s, _):
         xb_wait(s).wait_recv()
@@ -228,10 +291,11 @@
         return 0
     lax.fori_loop(0, 4, xwait_a, 0)
 
-    def rs_copy(t, ib):
-        to = partner(me, 6 - 2 * t)
-        at = pl.ds(pl.multiple_of(ib * GROUP, GROUP), GROUP)
-        return remote(rt.at[t, at], rs_recv.at[t, at], rs_ssem.at[t * 2 + ib], rs_rsem.at[t * 2 + ib], to)
+    def rs_copy(n):
+        t, ib, k = ((0, 0, 2), (0, 1, 4), (1, 0, 2), (2, 1, 4), (2, 0, 4), (1, 1, 2))[n]
+        at = pl.ds(ib * GROUP, GROUP)
+        dst = rs_mid.at[ib] if t == 0 else rs_recv.at[t - 1, at]
+        return remote(rt.at[t, at], dst, rs_ssem.at[n], rs_rsem.at[n], partner(me, k))
 
     def contract(o_s, tm):
         def outer(left, right_of):
@@ -244,8 +308,9 @@
             lax.fori_loop(0, 32 // QSTEP, qstep, 0)
 
         def eblk(n, _):
-            t, ib = n // 2, n % 2
-            c = partner(me, 6 - 2 * t) // 2
+            t = ((n // 2 + 1) // 2) % 2 * (1 + (n // 2 + n + 1) % 2) + 3 * (n // 6)
+            ib = n % 2
+            c = partner(me, 2 * (1 - t // 2) + 4 * (1 - t % 2)) // 2
             at = pl.ds(pl.multiple_of((c * rows + ib * GROUP) * 32, GROUP * 32), GROUP * 32)
             outer(lambda: a_all[at, :], lambda q: b_all[q])
 
@@ -256,9 +321,21 @@
                 return 0
             lax.fori_loop(0, GROUP // RSTEP, rstep, 0)
 
-            @pl.when(t < 3)
-            def _():
-                rs_copy(t, ib).start()
+            for v in range(6):
+                @pl.when(n == v)
+                def _():
+                    if v >= 4:
+                        rs_copy(v - 4).wait_recv()
+
+                        def add(i, _):
+                            at = (t, ib * GROUP + i)
+                            rt[at] = (rt[at].astype(F32) + rs_mid[v - 4, i].astype(F32)).astype(BF)
+                            return 0
+                        lax.fori_loop(0, GROUP, add, 0)
+                    rs_copy(v).start()
+                    if v == 1:
+                        for k in (2, 4, 3, 5, 6, 7):
+                            m_copy(k).start()
             return 0
         lax.fori_loop(0, 8, eblk, 0)
 
@@ -297,8 +374,8 @@
             z_copy(0).start()
             for j in range(rows // 8):
                 if j % 2 == 0:
-                    for t in range(3):
-                        rs_copy(t, j // 2).wait_recv()
+                    for n in ((2, 4), (3, 5))[j // 2]:
+                        rs_copy(n).wait_recv()
                 r_copy(j).start()
                 if j >= 1:
                     o_copy(j - 1).wait()
@@ -309,7 +386,7 @@
 
                 def row(i, _):
                     n = j * 8 + i
-                    tot = rt[3, n].astype(F32) + rb[0, i].astype(F32) + rb[1, i].astype(F32) + rb[2, i].astype(F32)
+                    tot = rt[3, n].astype(F32) + rb[0, i].astype(F32) + rb[1, i].astype(F32)
                     te = (tot + bo_e[...]) / (NORM_EPS + cnt_e[n])
                     zb[j % 2, i] = (zb[j % 2, i] + te.T) + tm[n].T
                     return 0
@@ -317,7 +394,7 @@
                 o_copy(j).start()
             o_copy(rows // 8 - 1).wait()
 
-        pl.run_scoped(final, pltpu.VMEM((2, 8, res, 128), F32), pltpu.VMEM((3, 8, 128, res), BF))
+        pl.run_scoped(final, pltpu.VMEM((2, 8, res, 128), F32), pltpu.VMEM((2, 8, 128, res), BF))
 
     pl.run_scoped(contract, pltpu.VMEM((GROUP, 1024, res), BF), pltpu.VMEM((rows, 128, res), F32))
 
@@ -339,16 +416,8 @@
         g_copy(i).wait_send()
     for i in range(3):
         f_copy(i).wait_send()
-        for ib in range(2):
-            rs_copy(i, ib).wait_send()
-
-
-def pair_counts(mask_rows, mask_full):
-    return jnp.einsum('si,sj->ij', mask_rows.astype(BF), mask_full.astype(BF), preferred_element_type=F32)
-
-
-def column(v):
-    return v.astype(F32)[:, None]
+    for n in range(6):
+        rs_copy(n).wait_send()
 
 
 def solution(mesh):
@@ -364,26 +433,10 @@
         res = extra_mask.shape[1]
         hid = e_wl.shape[1]
         nk = e_wo.shape[1]
-        me = lax.axis_index('dap')
         seq = seqs // 8
-
-        def counts(mask):
-            return pair_counts(lax.dynamic_slice_in_dim(mask, me * rows, rows, axis=1), mask)[:, None, :]
-
-        eye = jnp.eye(GROUP, dtype=BF)
-        w_b = (e_wr.T[:, None, None, :] * eye[None, :, :, None]).reshape(hid * GROUP, GROUP * ce)
-        w_a = (e_wl.T[None, :, None, :] * eye[:, None, :, None]).reshape(hid * GROUP, GROUP * ce)
-        w_blk = jnp.concatenate([w_b, w_a], axis=0)
-        bias_b = jnp.repeat(e_br.astype(F32), GROUP)[:, None]
-
-        def w_out_t(w):
-            return w.reshape(hid, hid, nk).transpose(2, 1, 0).reshape(nk, hid * hid)
-
         args = (
             jnp.transpose(extra_block, (1, 2, 0)), main_block, extra_mask, main_mask, pair_rows,
-            column(e_gam), column(e_bet), w_blk, bias_b, column(e_bl), w_out_t(e_wo), column(e_bo), counts(extra_mask),
-            m_gam.astype(F32)[None], m_bet.astype(F32)[None], jnp.concatenate([m_wl.T, m_wr.T], axis=0),
-            column(jnp.concatenate([m_bl, m_br])), w_out_t(m_wo), column(m_bo), counts(main_mask))
+            e_gam, e_bet, e_wl.T, e_bl, e_wr.T, e_br, e_wo, e_bo, m_gam, m_bet, m_wl.T, m_bl, m_wr.T, m_br, m_wo, m_bo)
         any_spec = pl.BlockSpec(memory_space=pl.ANY)
         vmem = pl.BlockSpec(memory_space=pltpu.VMEM)
         dma = pltpu.SemaphoreType.DMA
@@ -393,8 +446,8 @@
                 jax.ShapeDtypeStruct((rows, res, nk), F32),
                 jax.ShapeDtypeStruct((res, ce, seq), BF),
                 jax.ShapeDtypeStruct((mseqs // 8, res, cm), BF),
-                jax.ShapeDtypeStruct((3, rows, nk, res), BF)),
-            in_specs=[any_spec, any_spec, any_spec, vmem, any_spec] + [vmem] * 15,
+                jax.ShapeDtypeStruct((2, rows, nk, res), BF)),
+            in_specs=[any_spec, any_spec, any_spec, vmem, any_spec] + [vmem] * 16,
             out_specs=(any_spec,) * 4,
             scratch_shapes=[
                 pltpu.VMEM((4 * rows * hid, 2 * seq), BF),
@@ -404,11 +457,24 @@
                 pltpu.VMEM((GROUP * ce, seq), BF),
                 pltpu.VMEM((seq, res), jnp.int32),
                 pltpu.VMEM((res, seq), F32),
-                pltpu.VMEM((res, mseqs), F32),
                 pltpu.VMEM((rows, 1, mseqs), F32),
                 pltpu.VMEM((rows * hid, mseqs), BF),
                 pltpu.VMEM((hid, res, mseqs), BF),
                 pltpu.VMEM((4, rows, nk, res), BF),
+                pltpu.VMEM((2, GROUP, nk, res), BF),
+                pltpu.VMEM((2 * hid * GROUP, ce * GROUP), BF),
+                pltpu.VMEM((2 * hid, cm), BF),
+                pltpu.VMEM((nk, hid * hid), BF),
+                pltpu.VMEM((nk, hid * hid), BF),
+                pltpu.VMEM((ce, 1), F32),
+                pltpu.VMEM((ce, 1), F32),
+                pltpu.VMEM((hid * GROUP, 1), F32),
+                pltpu.VMEM((hid, 1), F32),
+                pltpu.VMEM((nk, 1), F32),
+                pltpu.VMEM((2 * hid, 1), F32),
+                pltpu.VMEM((nk, 1), F32),
+                pltpu.VMEM((rows, 1, res), F32),
+                pltpu.VMEM((rows, 1, res), F32),
                 dma((8,)), dma((8,)), dma((8,)), dma((8,)), dma((4,)), dma((4,)), dma((8,)), dma((8,)),
                 dma((4,)), dma((4,)), dma((3,)), dma((3,)), dma((6,)), dma((6,)), dma((8,))],
             compiler_params=pltpu.CompilerParams(

time: 371 us -> 327 us (0.88)
  Pallas kernels: 317 us -> 300 us
  local copies, waits for them, and re-layouts: 37.7 us -> 24.8 us
  other arithmetic: 11.1 us -> 0 us
    pallas_call x1, Pallas kernels: 317 us -> 300 us  [local_program(): pl.pallas_call(opm_kernel, out_shape=(jax.ShapeDtypeStruct((rows, res, nk...]
    broadcast_in_dim x7 -> x0, other arithmetic: 5.84 us -> none  [the longest x5 3.35 us: column(): return v.astype(F32)[:, None]]
    broadcast_in_dim x8 -> x0, local copies, waits for them, and re-layouts: 5.59 us -> none  [the longest x5 3.57 us: column(): return v.astype(F32)[:, None]]
    concatenate x2 -> x0, other arithmetic: 4.06 us -> none  [the longest x1 2.71 us: local_program(): w_blk = jnp.concatenate([w_b, w_a], axis=0)]
    mul x2 -> x0, local copies, waits for them, and re-layouts: 3.76 us -> none  [the longest x1 2.28 us: local_program(): e_wr.T[:, None, None, :] * eye[None, :, :, None]]
    unnamed x15 -> x5, local copies, waits for them, and re-layouts: 24.8 us -> 24.8 us
where the time goes in v2:
time: 327 us; the launch traced here: 326 us
  Pallas kernels  300 us (92%)
  local copies, waits for them, and re-layouts  24.8 us (8%)
    pallas_call x1, Pallas kernels, local_program(): pl.pallas_call(opm_kernel, out_shape=(jax.ShapeDtypeStruct((rows, res, nk...  300 us
    unnamed x5, local copies, waits for them, and re-layouts  24.8 us

profile of v2, /device:TPU:0, one launch (start us, length us, event | category | flops | bytes accessed | tf_op | source)
XLA Modules:
  0.0 325.6 jit_solution(1807741155693967682)
XLA Ops:
  0.6 300.1 %opm.1 = (f32[32,256,128]{2,1,0:T(8,128)}, bf16[256,64,384]{2,1,0:T(8,128)(2,1)}, bf16[32,256,256]{2,1,0:T(8,128)(2,1)}, bf16[2,32,128,256]{3,2,1,0:T(8,128)(2,1)}) custom-call(bf16[32,64,3072]{2,1,0:T(8,128)(2,1)} %bitcast.6, bf16[256,32,256]{2,1,0:T(8,128)(2,1)} %xm.1, s32[3072,256]{1,0:T(8,128)} %mask_e.1, s32[256,256]{1,0:T(8,128)} %mask_m.1, ...), custom_call_target="tpu_custom_call" | custom-call | tf_op jit(solution)/shard_map/opm/pallas_call | solution.py:443
  300.8 18.0 %copy.24 = bf16[384,256,64]{1,2,0:T(8,128)(2,1)} copy(bf16[384,256,64]{0,2,1:T(8,128)(2,1)} %bitcast.7) | data formatting | bytes 25165824
  318.8 0.0 copy-start
  318.8 4.8 %copy.27 = f32[32,256,128]{2,1,0:T(8,128)} copy(f32[32,256,128]{2,1,0:T(8,128)} %get-tuple-element.15) | data formatting | bytes 8388608
  323.6 0.0 copy-done
  323.6 2.0 copy.28
Async XLA Ops:
  318.8 4.8 %copy-start = (bf16[32,256,256]{2,1,0:T(8,128)(2,1)S(1)}, bf16[32,256,256]{2,1,0:T(8,128)(2,1)}, u32[]{:S(2)}) copy-start(bf16[32,256,256]{2,1,0:T(8,128)(2,1)} %get-tuple-element.17) | copy-start | bytes 12582916

commit v3 on v2

v3 whole, which is shorter than its diff:
```python
import functools

import jax
import jax.numpy as jnp
from jax import lax
from jax.experimental import pallas as pl
from jax.experimental.pallas import tpu as pltpu
from jax.sharding import PartitionSpec as P

LN_EPS = 1e-5
NORM_EPS = 1e-3
BF = jnp.bfloat16
F32 = jnp.float32
GROUP = 16
QSTEP = 4
LSTEP = 4
MSTEP = 8
RG, LG = 8, 4
HID, CE, LANES, HALF = 32, 64, 128, 64
RSTEP = 8


def loop(n, body):
    def step(i, carry):
        body(i)
        return carry
    lax.fori_loop(0, n, step, 0)


def part(i, n):
    return pl.ds(pl.multiple_of(i * n, n), n)


def partner(me, k):
    core, cx, cy = me % 2, (me // 2) % 2, me // 4
    k0, k1, k2 = k % 2, (k // 2) % 2, k // 4
    return (core + k0) % 2 + 2 * ((cx + k1) % 2) + 4 * ((cy + k2) % 2)


def nt_dot(lhs, rhs):
    return lax.dot_general(lhs, rhs, (((1,), (1,)), ((), ())), preferred_element_type=F32)


def column(row, n, repeat):
    m = row.shape[1]
    at = lax.broadcasted_iota(jnp.int32, (n, m), 0) // repeat
    return jnp.sum(jnp.where(at == lax.broadcasted_iota(jnp.int32, (n, m), 1), row, 0.0), axis=1, keepdims=True)


def opm_kernel(
    xe, xm, mask_e, mask_m, pair,
    e_gam, e_bet, e_wl, e_bl, e_wr, e_br, e_wo, e_bo,
    m_gam, m_bet, m_wl, m_bl, m_wr, m_br, m_wo, m_bo,
    pair_out, e_out, m_out,
    a_all, b_all, a_send, xb, y_s, mask_i, mask_et, mask_mo, am, bm, rt, rs_mid, rs_recv, r_own,
    w_right, w_left, w_m, wo_e, wo_m, gam_e, bet_e, bias_b, bias_a, bo_e, bias_m, bo_m, cnt_e, cnt_m,
    e_ssem, e_rsem, m_ssem, m_rsem, xa_ssem, xa_rsem, xb_ssem, xb_rsem,
    g_ssem, g_rsem, f_ssem, f_rsem, rs_ssem, rs_rsem, ob_ssem, ob_rsem, ob_free, lsem,
):
    me = lax.axis_index('dap')
    core = me % 2
    chip = me // 2
    sib = partner(me, 1)
    seq = e_out.shape[2]
    mseq = m_out.shape[0]
    rows = xe.shape[0]
    res = e_out.shape[0]

    def dev(d):
        return {'dap': d}

    def lane(h):
        return pl.ds(pl.multiple_of(h * seq, LANES), seq)

    def rblk(d, n=rows):
        return part(d, n)

    barrier = pltpu.get_barrier_semaphore()
    for k in range(1, 8):
        pl.semaphore_signal(barrier, inc=1, device_id=dev(partner(me, k)), device_id_type=pl.DeviceIdType.MESH)
    pl.semaphore_wait(barrier, 7)

    def remote(src, dst, ssem, rsem, target):
        return pltpu.make_async_remote_copy(
            src_ref=src, dst_ref=dst, send_sem=ssem, recv_sem=rsem,
            device_id=dev(target), device_id_type=pl.DeviceIdType.MESH)

    def e_copy(k):
        to = partner(me, k)
        return remote(xe.at[:, :, lane(to)], e_out.at[rblk(me)], e_ssem.at[k], e_rsem.at[k], to)

    for k in (1, 2, 4, 3, 5, 6, 7):
        e_copy(k).start()

    def m_copy(k):
        to = partner(me, k)
        return remote(xm.at[rblk(to, mseq)], m_out.at[:, rblk(me), :], m_ssem.at[k], m_rsem.at[k], to)

    def row_of(ref):
        v = ref[:].astype(F32)
        return v.reshape(1, v.shape[0])

    def weights(wf, wp):
        gam_e[:] = column(row_of(e_gam), HALF, 1)
        bet_e[:] = column(row_of(e_bet), HALF, 1)
        bias_b[:] = column(row_of(e_br), HID * RG, RG)
        bias_a[:] = column(row_of(e_bl), HID, 1)
        bo_e[:] = column(row_of(e_bo), LANES, 1)
        bo_m[:] = column(row_of(m_bo), LANES, 1)
        bias_m[:HID] = column(row_of(m_bl), HID, 1)
        bias_m[HID:] = column(row_of(m_br), HID, 1)
        w_m[:HID] = m_wl[:]
        w_m[HID:] = m_wr[:]

        def wide(ref, n):
            w = ref[:].astype(F32)
            return jnp.concatenate([w] * n, axis=1)

        def place(dst, rep, residue):
            at = lax.broadcasted_iota(jnp.int32, dst.shape, 0)
            dst[:] = jnp.where(residue(at) == lax.broadcasted_iota(jnp.int32, dst.shape, 1) // CE, rep, 0.0).astype(BF)

        w = wide(e_wr, RG)
        place(w_right, jnp.broadcast_to(w[:, None, :], (HID, RG, RG * CE)).reshape(HID * RG, RG * CE), lambda at: at % RG)
        place(w_left, jnp.concatenate([wide(e_wl, LG)] * LG, axis=0), lambda at: at // HID)
        for src, dst in ((e_wo, wo_e), (m_wo, wo_m)):
            wf[:] = src[:].astype(F32)

            def pick(q):
                wp[part(q, HID), :] = wf[pl.ds(q, HID, stride=HID), :]
            loop(HID, pick)
            dst[:] = wp[:].T.astype(BF)

    pl.run_scoped(weights, pltpu.VMEM((1024, LANES), F32), pltpu.VMEM((1024, LANES), F32))

    def masks(mt):
        mt[:] = mask_m[:].astype(F32).T
        own = mt[rblk(me), :]
        mask_mo[:] = own.reshape(rows, 1, mask_m.shape[0])
        cnt_m[:] = jnp.dot(own.astype(BF), mask_m[:].astype(F32).astype(BF),
                             preferred_element_type=F32).reshape(rows, 1, res)

    pl.run_scoped(masks, pltpu.VMEM((res, mask_m.shape[0]), F32))

    def load_mask(d):
        cp = pltpu.make_async_copy(mask_e.at[rblk(d, seq)], mask_i, lsem.at[0])
        cp.start()
        cp.wait()

    def main_proj(xc, xf, bf):
        cp = pltpu.make_async_copy(xm.at[rblk(me, mseq)], xc.at[pl.ds(0, mseq)], lsem.at[1])
        cp.start()
        cp.wait()
        cp = pltpu.make_async_copy(xc.at[pl.ds(0, mseq)], m_out.at[:, rblk(me), :], lsem.at[1])
        cp.start()
        cp.wait()
        step = xc.shape[0]
        gam_m, bet_m = row_of(m_gam), row_of(m_bet)
        for piece in range(xm.shape[0] // step):
            cp = pltpu.make_async_copy(xm.at[pl.ds(piece * step, step)], xc, lsem.at[2])
            cp.start()
            cp.wait()

            def widen(i):
                s = part(i, 8)
                xf[s] = xc[s].astype(F32)
            loop(step // 8, widen)

            def one(r):
                x = xf[:, r, :]
                mean = jnp.mean(x, axis=1, keepdims=True)
                cen = x - mean
                var = jnp.mean(cen * cen, axis=1, keepdims=True)
                y = (cen * lax.rsqrt(var + LN_EPS) * gam_m + bet_m).astype(BF)
                proj = nt_dot(w_m[:], y) + bias_m[:]
                proj = proj * mask_mo[r, :, pl.ds(piece * step, step)]
                am[part(r, HID), pl.ds(piece * step, step)] = proj[:HID].astype(BF)
                bf[:, r, :] = proj[HID:]
            def some(i):
                for u in range(MSTEP):
                    one(i * MSTEP + u)

            loop(rows // MSTEP, some)
            bm[:, rblk(me), pl.ds(piece * step, step)] = bf[:].astype(BF)

    pl.run_scoped(
        main_proj, pltpu.VMEM((LANES, rows, xm.shape[2]), BF), pltpu.VMEM((LANES, rows, xm.shape[2]), F32),
        pltpu.VMEM((HID, rows, LANES), F32))

    def g_copy(i):
        ref = bm.at[:, rblk(me), :]
        return remote(ref, ref, g_ssem.at[i], g_rsem.at[i], partner(me, (1, 2, 4, 6)[i]))

    def g_wait(i):
        to = partner(me, (1, 2, 4, 6)[i])
        ref = bm.at[:, rblk(to), :]
        return remote(ref, ref, g_ssem.at[i], g_rsem.at[i], to)

    def f_copy(i):
        ref = bm.at[:, rblk(partner(me, (2, 4, 6)[i])), :]
        return remote(ref, ref, f_ssem.at[i], f_rsem.at[i], sib)

    def f_wait(i):
        ref = bm.at[:, rblk(partner(me, (3, 5, 7)[i])), :]
        return remote(ref, ref, f_ssem.at[i], f_rsem.at[i], sib)

    for i in range(4):
        g_copy(i).start()
    for k in (1, 2, 4):
        m_copy(k).start()

    def project(hh, m16):
        def norm(i):
            for u in range(LSTEP):
                r = i * LSTEP + u
                x = xb[hh * GROUP + r].astype(F32)
                mean = jnp.mean(x, axis=0, keepdims=True)
                cen = x - mean
                var = jnp.mean(cen * cen, axis=0, keepdims=True)
                y = cen * lax.rsqrt(var + LN_EPS) * gam_e[:] + bet_e[:]
                y_s[part(r, CE), :] = y.astype(BF)
        loop(GROUP // LSTEP, norm)

        def dot(w, g):
            return jnp.dot(w[:], y_s[pl.ds(g * w.shape[1], w.shape[1])], preferred_element_type=F32)

        right = jnp.concatenate(
            [(dot(w_right, g) + bias_b[:]).reshape(HID, RG, seq) for g in range(GROUP // RG)], axis=1)
        right = (right * m16[None]).astype(BF)
        left = []
        for g in range(GROUP // LG):
            d = dot(w_left, g)
            for r in range(LG):
                left.append((d[r * HID:r * HID + HID] + bias_a[:]) * m16[g * LG + r:g * LG + r + 1])
        left = jnp.concatenate(left, axis=0).astype(BF)
        return right, left

    lane_lo = lax.broadcasted_iota(jnp.int32, (LANES, LANES), 1) < HALF

    def ob_copy(d, e, h):
        ref = rt.at[d % 4, :, pl.ds(pl.multiple_of(e * HALF + h * rows, rows), rows), :]
        return remote(ref, ref, ob_ssem.at[d % 4 * 2 + e], ob_rsem.at[d % 4 * 2 + e], sib)

    def own_pairs(mt, cnt, a_own, acc, o_pair):
        cnt[:] = jnp.zeros_like(cnt)

        def zero(g):
            acc[g] = jnp.zeros(acc.shape[1:], F32)
        loop(acc.shape[0], zero)

        def chunk(d):
            xcp = pltpu.make_async_copy(xe.at[:, :, lane(d)], xb, lsem.at[1])
            xcp.start()
            load_mask(d)
            m = mask_i[:].astype(F32)
            mt[:] = m.T
            cnt[:] += jnp.dot(mt[rblk(me), :].astype(BF), m.astype(BF), preferred_element_type=F32)

            @pl.when(d >= 4)
            def _():
                for e in range(2):
                    ob_copy(d, e, core).wait_send()
            xcp.wait()

            def half(hh):
                right, left = project(hh, mt[pl.ds(pl.multiple_of(me * rows + hh * GROUP, GROUP), GROUP), :])
                right = right.reshape(16, 2, GROUP, seq)
                for e in range(2):
                    at = pl.ds(pl.multiple_of(e * HALF + core * rows + hh * GROUP, GROUP), GROUP)
                    rt[d % 4, :, at, :] = right[:, e]
                a_own[d % 2, part(hh, GROUP * HID), :] = left
            loop(rows // GROUP, half)

            @pl.when((d // 4) * ((d + 1) % 2) == 1)
            def _():
                pl.semaphore_wait(ob_free, 1)
            for e in range(2):
                ob_copy(d, e, core).start()

            @pl.when(d % 2 == 1)
            def _():
                for e in range(2):
                    ob_copy(d - 1, e, 1 - core).wait_recv()
                    ob_copy(d, e, 1 - core).wait_recv()

                def group(g):
                    at = part(g, 2)
                    acc[g] += (nt_dot(a_own[0], rt[(d - 1) % 4, at].reshape(256, seq))
                               + nt_dot(a_own[1], rt[d % 4, at].reshape(256, seq)))
                loop(acc.shape[0], group)

                @pl.when(d < 4)
                def _():
                    pl.semaphore_signal(ob_free, inc=1, device_id=dev(sib), device_id_type=pl.DeviceIdType.MESH)
        loop(8, chunk)
        cnt_e[:] = cnt[:].reshape(rows, 1, res)

        def pair_rows(n):
            for g in range(8):
                t = acc[g, part(n, HALF), :]
                for b in range(2):
                    u0, u1 = t[:HID, b * LANES:b * LANES + LANES], t[HID:, b * LANES:b * LANES + LANES]
                    q = g * 4 + b * 2
                    lo = lane_lo[:HID]
                    o_pair[q * HID:q * HID + HID, :] = jnp.where(lo, u0, pltpu.roll(u1, HALF, 1)).astype(BF)
                    o_pair[q * HID + HID:q * HID + HALF, :] = jnp.where(lo, pltpu.roll(u0, HALF, 1), u1).astype(BF)
            r_own[n] = jnp.dot(wo_e[:], o_pair[:], preferred_element_type=F32)
        loop(rows // 2, pair_rows)
        for d in range(4, 8):
            for e in range(2):
                ob_copy(d, e, core).wait_send()
        load_mask(me)
        mask_et[:] = mask_i[:].astype(F32).T

    pl.run_scoped(
        own_pairs, pltpu.VMEM((res, seq), F32), pltpu.VMEM((rows, res), F32),
        pltpu.VMEM((2, rows * HID, seq), BF), pltpu.VMEM((8, rows * HID, 256), F32), pltpu.VMEM((1024, LANES), BF))

    def xb_copy(src):
        ref = b_all.at[:, rblk(src), lane(core)]
        return remote(ref, ref, xb_ssem.at[src], xb_rsem.at[src], sib)

    def xb_wait(src):
        ref = b_all.at[:, rblk(src), lane(1 - core)]
        return remote(ref, ref, xb_ssem.at[src], xb_rsem.at[src], sib)

    def xa_copy(c):
        return remote(a_send.at[rblk(c, rows * HID)], a_all.at[rblk(c, rows * HID), lane(core)],
                      xa_ssem.at[c], xa_rsem.at[c], sib)

    def xa_wait(c):
        return remote(a_send.at[rblk(c, rows * HID)], a_all.at[rblk(c, rows * HID), lane(1 - core)],
                      xa_ssem.at[c], xa_rsem.at[c], sib)

    def block(k):
        src = partner(me, k)
        own_half = (src % 2 + core) % 2

        @pl.when(k == 0)
        def _():
            cp = pltpu.make_async_copy(xe.at[:, :, lane(me)], xb, lsem.at[0])
            cp.start()
            cp.wait()
            cp = pltpu.make_async_copy(xb, e_out.at[rblk(me)], lsem.at[0])
            cp.start()
            cp.wait()

        @pl.when(k > 0)
        def _():
            remote(xe.at[:, :, lane(src)], e_out.at[rblk(src)], e_ssem.at[k], e_rsem.at[k], src).wait_recv()
            cp = pltpu.make_async_copy(e_out.at[rblk(src)], xb, lsem.at[0])
            cp.start()
            cp.wait()

        def half(hh):
            r0 = pl.multiple_of(src * rows + hh * GROUP, GROUP)
            right, left = project(hh, mask_et[pl.ds(r0, GROUP), :])
            b_all[:, pl.ds(r0, GROUP), lane(core)] = right
            at = pl.ds(pl.multiple_of(((src // 2) * rows + hh * GROUP) * HID, GROUP * HID), GROUP * HID)

            @pl.when(own_half == 0)
            def _():
                a_all[at, lane(core)] = left

            @pl.when(own_half == 1)
            def _():
                a_send[at, :] = left
        loop(rows // GROUP, half)
        xb_copy(src).start()

        @pl.when(own_half == 1)
        def _():
            xa_copy(src // 2).start()
    loop(8, block)

    for k in range(1, 8):
        e_copy(k).wait_send()


    def xwait(s):
        xb_wait(s).wait_recv()
    loop(8, xwait)

    def xwait_a(c):
        xa_wait(c).wait_recv()
    loop(4, xwait_a)

    def rs_copy(n):
        t, ib, k = ((0, 0, 2), (0, 1, 4), (1, 0, 2), (2, 1, 4), (2, 0, 4), (1, 1, 2))[n]
        at = pl.ds(ib * GROUP // 2, GROUP // 2)
        dst = rs_mid.at[ib] if t == 0 else rs_recv.at[t - 1, at]
        return remote(rt.at[t, at], dst, rs_ssem.at[n], rs_rsem.at[n], partner(me, k))

    def contract(o_s, tm):
        def outer(left, right_of):
            def qstep(qq):
                for u in range(QSTEP):
                    q = qq * QSTEP + u
                    o = nt_dot(left(), right_of(q))
                    o_s[:, part(q, HID), :] = o.astype(BF).reshape(GROUP, HID, res)
            loop(HID // QSTEP, qstep)

        def eblk(n):
            t = ((n // 2 + 1) // 2) % 2 * (1 + (n // 2 + n + 1) % 2) + 3 * (n // 6)
            ib = n % 2
            c = partner(me, 2 * (1 - t // 2) + 4 * (1 - t % 2)) // 2
            at = pl.ds(pl.multiple_of((c * rows + ib * GROUP) * HID, GROUP * HID), GROUP * HID)
            outer(lambda: a_all[at, :], lambda q: b_all[q])

            hi0 = lax.broadcasted_iota(jnp.int32, (LANES, LANES), 0) * 0 + c // 2 == 0
            odd = lax.broadcasted_iota(jnp.int32, (LANES, LANES), 0) * 0 + c % 2 == 1

            def rstep(ii):
                for u in range(RSTEP // 2):
                    n2 = ii * (RSTEP // 2) + u
                    away, near = [], []
                    for v in range(2):
                        r = jnp.dot(wo_e[:], o_s[n2 * 2 + v], preferred_element_type=F32)
                        away.append(jnp.where(hi0, r[:, LANES:], r[:, :LANES]))
                        near.append(jnp.where(hi0, r[:, :LANES], r[:, LANES:]))
                    n0 = jnp.where(odd, near[0], pltpu.roll(near[0], HALF, 1))
                    n1 = jnp.where(odd, pltpu.roll(near[1], HALF, 1), near[1])
                    rt[t, ib * (GROUP // 2) + n2] = jnp.concatenate(
                        [away[0], away[1], jnp.where(lane_lo, n0, n1)], axis=1).astype(BF)
            loop(GROUP // RSTEP, rstep)

            for v in range(6):
                @pl.when(n == v)
                def _():
                    if v >= 4:
                        rs_copy(v - 4).wait_recv()

                        def add(i):
                            at = (t, ib * (GROUP // 2) + i)
                            rt[at] = (rt[at].astype(F32) + rs_mid[v - 4, i].astype(F32)).astype(BF)
                        loop(GROUP // 2, add)
                    rs_copy(v).start()
                    if v == 1:
                        for k in (3, 5, 6, 7):
                            m_copy(k).start()
        loop(8, eblk)

        for i in range(1, 4):
            g_wait(i).wait_recv()
            f_copy(i - 1).start()
        g_wait(0).wait_recv()
        for i in range(3):
            f_wait(i).wait_recv()

        def mblk(ib):
            at = part(ib, GROUP * HID)
            outer(lambda: am[at, :], lambda q: bm[q])

            def rstep(ii):
                for u in range(RSTEP):
                    i = ii * RSTEP + u
                    row = ib * GROUP + i
                    r = jnp.dot(wo_m[:], o_s[i], preferred_element_type=F32)
                    tm[row] = (r + bo_m[:]) / (NORM_EPS + cnt_m[row])
            loop(GROUP // RSTEP, rstep)
        loop(rows // GROUP, mblk)

        def final(zb):
            def z_copy(j):
                return pltpu.make_async_copy(pair.at[pl.ds(j * 8, 8)], zb.at[j % 2], lsem.at[3 + j % 2])

            def o_copy(j):
                return pltpu.make_async_copy(zb.at[j % 2], pair_out.at[pl.ds(j * 8, 8)], lsem.at[5 + j % 2])

            hi0 = lax.broadcasted_iota(jnp.int32, (LANES, LANES), 0) * 0 + chip // 2 == 0
            odd = lax.broadcasted_iota(jnp.int32, (LANES, LANES), 0) * 0 + chip % 2 == 1
            z_copy(0).start()
            for j in range(rows // 8):
                if j % 2 == 0:
                    for n in ((2, 4), (3, 5))[j // 2]:
                        rs_copy(n).wait_recv()
                if j >= 1:
                    o_copy(j - 1).wait()
                if j + 1 < rows // 8:
                    z_copy(j + 1).start()
                z_copy(j).wait()

                def row2(i):
                    n = j * 4 + i
                    tot = rt[3, n].astype(F32) + rs_recv[0, n].astype(F32) + rs_recv[1, n].astype(F32)
                    kept, own = tot[:, 256:], r_own[n]
                    rkept, rown = pltpu.roll(kept, HALF, 1), pltpu.roll(own, HALF, 1)
                    near0 = jnp.where(lane_lo, jnp.where(odd, kept, own), jnp.where(odd, rown, rkept))
                    near1 = jnp.where(lane_lo, jnp.where(odd, rkept, rown), jnp.where(odd, own, kept))
                    for v, near in ((0, near0), (1, near1)):
                        away = tot[:, v * LANES:v * LANES + LANES]
                        row = n * 2 + v
                        r = jnp.concatenate([jnp.where(hi0, near, away), jnp.where(hi0, away, near)], axis=1)
                        te = (r + bo_e[:]) / (NORM_EPS + cnt_e[row])
                        zb[j % 2, i * 2 + v] = (zb[j % 2, i * 2 + v] + te.T) + tm[row].T
                loop(4, row2)
                o_copy(j).start()
            o_copy(rows // 8 - 1).wait()

        pl.run_scoped(final, pltpu.VMEM((2, 8, res, LANES), F32))

    pl.run_scoped(contract, pltpu.VMEM((GROUP, 1024, res), BF), pltpu.VMEM((rows, LANES, res), F32))

    for k in range(1, 8):
        m_copy(k).wait_send()
        to = partner(me, k)
        remote(xm.at[rblk(me, mseq)], m_out.at[:, rblk(to), :], m_ssem.at[k], m_rsem.at[k], to).wait_recv()

    def drain(s):
        xb_copy(s).wait_send()
    loop(8, drain)

    def drain_a(c):
        xa_copy(c).wait_send()
    loop(4, drain_a)
    for i in range(4):
        g_copy(i).wait_send()
    for i in range(3):
        f_copy(i).wait_send()
    for n in range(6):
        rs_copy(n).wait_send()


def solution(mesh):
    msa_spec = P('data', 'dap', None)
    mask_spec = P('data', None)
    row_spec = P(('data', 'dap'), None, None)

    def local_program(extra_block, extra_mask, main_block, main_mask, pair_rows,
                      e_gam, e_bet, e_wl, e_bl, e_wr, e_br, e_wo, e_bo,
                      m_gam, m_bet, m_wl, m_bl, m_wr, m_br, m_wo, m_bo):
        seqs, rows, ce = extra_block.shape
        mseqs, _, cm = main_block.shape
        res = extra_mask.shape[1]
        hid = e_wl.shape[1]
        nk = e_wo.shape[1]
        seq = seqs // 8
        args = (
            jnp.transpose(extra_block, (1, 2, 0)), main_block, extra_mask, main_mask, pair_rows,
            e_gam, e_bet, e_wl.T, e_bl, e_wr.T, e_br, e_wo, e_bo, m_gam, m_bet, m_wl.T, m_bl, m_wr.T, m_br, m_wo, m_bo)
        any_spec = pl.BlockSpec(memory_space=pl.ANY)
        vmem = pl.BlockSpec(memory_space=pltpu.VMEM)
        dma = pltpu.SemaphoreType.DMA
        pair_out, e_recv, m_recv = pl.pallas_call(
            opm_kernel,
            out_shape=(
                jax.ShapeDtypeStruct((rows, res, nk), F32),
                jax.ShapeDtypeStruct((res, ce, seq), BF),
                jax.ShapeDtypeStruct((mseqs // 8, res, cm), BF)),
            in_specs=[any_spec, any_spec, any_spec, vmem, any_spec] + [vmem] * 16,
            out_specs=(any_spec,) * 3,
            scratch_shapes=[
                pltpu.VMEM((4 * rows * hid, 2 * seq), BF),
                pltpu.VMEM((hid, res, 2 * seq), BF),
                pltpu.VMEM((4 * rows * hid, seq), BF),
                pltpu.VMEM((rows, ce, seq), BF),
                pltpu.VMEM((GROUP * ce, seq), BF),
                pltpu.VMEM((seq, res), jnp.int32),
                pltpu.VMEM((res, seq), F32),
                pltpu.VMEM((rows, 1, mseqs), F32),
                pltpu.VMEM((rows * hid, mseqs), BF),
                pltpu.VMEM((hid, res, mseqs), BF),
                pltpu.VMEM((4, rows // 2, nk, res // 2 * 3), BF),
                pltpu.VMEM((2, GROUP // 2, nk, res // 2 * 3), BF),
                pltpu.VMEM((2, rows // 2, nk, res // 2 * 3), BF),
                pltpu.VMEM((rows // 2, nk, res // 2), F32),
                pltpu.VMEM((hid * RG, ce * RG), BF),
                pltpu.VMEM((hid * LG, ce * LG), BF),
                pltpu.VMEM((2 * hid, cm), BF),
                pltpu.VMEM((nk, hid * hid), BF),
                pltpu.VMEM((nk, hid * hid), BF),
                pltpu.VMEM((ce, 1), F32),
                pltpu.VMEM((ce, 1), F32),
                pltpu.VMEM((hid * RG, 1), F32),
                pltpu.VMEM((hid, 1), F32),
                pltpu.VMEM((nk, 1), F32),
                pltpu.VMEM((2 * hid, 1), F32),
                pltpu.VMEM((nk, 1), F32),
                pltpu.VMEM((rows, 1, res), F32),
                pltpu.VMEM((rows, 1, res), F32),
                dma((8,)), dma((8,)), dma((8,)), dma((8,)), dma((4,)), dma((4,)), dma((8,)), dma((8,)),
                dma((4,)), dma((4,)), dma((3,)), dma((3,)), dma((6,)), dma((6,)),
                dma((8,)), dma((8,)), pltpu.SemaphoreType.REGULAR, dma((8,))],
            compiler_params=pltpu.CompilerParams(
                collective_id=0, has_side_effects=True, vmem_limit_bytes=67043328),
            name='opm',
        )(*args)
        return pair_out, jnp.transpose(e_recv, (2, 0, 1)), m_recv

    in_specs = (msa_spec, mask_spec, msa_spec, mask_spec, row_spec) + (P(),) * 16
    return jax.shard_map(local_program, mesh=mesh, in_specs=in_specs, out_specs=(row_spec,) * 3, check_vma=False)
```

time: 327 us -> 298 us (0.911)
  Pallas kernels: 300 us -> 271 us
    pallas_call x1, Pallas kernels: 300 us -> 271 us  [local_program(): pl.pallas_call(opm_kernel, out_shape=(jax.ShapeDtypeStruct((rows, res, nk...]
where the time goes in v3:
time: 298 us; the launch traced here: 297 us
  Pallas kernels  271 us (91%)
  local copies, waits for them, and re-layouts  24.8 us (8%)
    pallas_call x1, Pallas kernels, local_program(): pl.pallas_call(opm_kernel, out_shape=(jax.ShapeDtypeStruct((rows, res, nk...  271 us
    unnamed x5, local copies, waits for them, and re-layouts  24.8 us

profile of v3, /device:TPU:0, one launch (start us, length us, event | category | flops | bytes accessed | tf_op | source)
XLA Modules:
  0.0 296.6 jit_solution(1470494674871265475)
XLA Ops:
  0.6 271.2 %opm.1 = (f32[32,256,128]{2,1,0:T(8,128)}, bf16[256,64,384]{2,1,0:T(8,128)(2,1)}, bf16[32,256,256]{2,1,0:T(8,128)(2,1)}) custom-call(bf16[32,64,3072]{2,1,0:T(8,128)(2,1)} %bitcast.6, bf16[256,32,256]{2,1,0:T(8,128)(2,1)} %xm.1, s32[3072,256]{1,0:T(8,128)} %mask_e.1, s32[256,256]{1,0:T(8,128)} %mask_m.1, f32[32,256,128]{2,1,0:T(8,128)} %pair.1, ...), custom_call_target="tpu_custom_call" | custom-call | tf_op jit(solution)/shard_map/opm/pallas_call | solution.py:544
  271.8 18.0 %copy.24 = bf16[384,256,64]{1,2,0:T(8,128)(2,1)} copy(bf16[384,256,64]{0,2,1:T(8,128)(2,1)} %bitcast.7) | data formatting | bytes 25165824
  289.8 0.0 copy-start
  289.8 4.8 %copy.27 = f32[32,256,128]{2,1,0:T(8,128)} copy(f32[32,256,128]{2,1,0:T(8,128)} %get-tuple-element.15) | data formatting | bytes 8388608
  294.6 0.0 copy-done
  294.6 2.0 copy.28
Async XLA Ops:
  289.8 4.8 %copy-start = (bf16[32,256,256]{2,1,0:T(8,128)(2,1)S(1)}, bf16[32,256,256]{2,1,0:T(8,128)(2,1)}, u32[]{:S(2)}) copy-start(bf16[32,256,256]{2,1,0:T(8,128)(2,1)} %get-tuple-element.17) | copy-start | bytes 12582916

commit v4 on v3

--- a/solution.py
+++ b/solution.py
@@ -12,6 +12,7 @@
 BF = jnp.bfloat16
 F32 = jnp.float32
 GROUP = 16
+VMEM_LIMIT = 58 * 2 ** 20
 QSTEP = 4
 LSTEP = 4
 MSTEP = 8
@@ -51,11 +52,11 @@
     xe, xm, mask_e, mask_m, pair,
     e_gam, e_bet, e_wl, e_bl, e_wr, e_br, e_wo, e_bo,
     m_gam, m_bet, m_wl, m_bl, m_wr, m_br, m_wo, m_bo,
-    pair_out, e_out, m_out,
+    pair_out, e_t, m_out, e_out,
     a_all, b_all, a_send, xb, y_s, mask_i, mask_et, mask_mo, am, bm, rt, rs_mid, rs_recv, r_own,
     w_right, w_left, w_m, wo_e, wo_m, gam_e, bet_e, bias_b, bias_a, bo_e, bias_m, bo_m, cnt_e, cnt_m,
     e_ssem, e_rsem, m_ssem, m_rsem, xa_ssem, xa_rsem, xb_ssem, xb_rsem,
-    g_ssem, g_rsem, f_ssem, f_rsem, rs_ssem, rs_rsem, ob_ssem, ob_rsem, ob_free, lsem,
+    d_ssem, d_rsem, t_isem, t_osem, g_ssem, g_rsem, f_ssem, f_rsem, rs_ssem, rs_rsem, ob_ssem, ob_rsem, ob_free, lsem,
 ):
     me = lax.axis_index('dap')
     core = me % 2
@@ -189,12 +190,20 @@
 
     def g_copy(i):
         ref = bm.at[:, rblk(me), :]
-        return remote(ref, ref, g_ssem.at[i], g_rsem.at[i], partner(me, (1, 2, 4, 6)[i]))
+        return remote(ref, ref, g_ssem.at[i], g_rsem.at[i], partner(me, (1, 2, 4)[i]))
 
     def g_wait(i):
-        to = partner(me, (1, 2, 4, 6)[i])
+        to = partner(me, (1, 2, 4)[i])
         ref = bm.at[:, rblk(to), :]
         return remote(ref, ref, g_ssem.at[i], g_rsem.at[i], to)
+
+    def d_copy(i):
+        ref = bm.at[part(i, HID // 2), rblk(partner(me, (2, 4)[i])), :]
+        return remote(ref, ref, d_ssem.at[i], d_rsem.at[i], partner(me, (4, 2)[i]))
+
+    def d_wait(i):
+        ref = bm.at[part(i, HID // 2), rblk(partner(me, 6)), :]
+        return remote(ref, ref, d_ssem.at[i], d_rsem.at[i], partner(me, (4, 2)[i]))
 
     def f_copy(i):
         ref = bm.at[:, rblk(partner(me, (2, 4, 6)[i])), :]
@@ -204,7 +213,7 @@
         ref = bm.at[:, rblk(partner(me, (3, 5, 7)[i])), :]
         return remote(ref, ref, f_ssem.at[i], f_rsem.at[i], sib)
 
-    for i in range(4):
+    for i in range(3):
         g_copy(i).start()
     for k in (1, 2, 4):
         m_copy(k).start()
@@ -316,6 +325,52 @@
         own_pairs, pltpu.VMEM((res, seq), F32), pltpu.VMEM((rows, res), F32),
         pltpu.VMEM((2, rows * HID, seq), BF), pltpu.VMEM((8, rows * HID, 256), F32), pltpu.VMEM((1024, LANES), BF))
 
+    def transpose(yh):
+        def body(tin, tout, f_in, f_out):
+            side = GROUP * 8
+
+            def i_copy(u):
+                return pltpu.make_async_copy(
+                    e_out.at[part(yh, side), part(u % 4, GROUP), part(u // 4, side)], tin.at[u % 2], t_isem.at[u % 2])
+
+            def o_copy(u):
+                return pltpu.make_async_copy(
+                    tout.at[u % 2], e_t.at[part(u // 4, side), part(u % 4, GROUP), part(yh, side)], t_osem.at[u % 2])
+
+            i_copy(0).start()
+
+            def unit(u):
+                @pl.when(u < 11)
+                def _():
+                    i_copy(u + 1).start()
+                i_copy(u).wait()
+
+                def widen(i):
+                    f_in[part(i, side)] = tin[u % 2, part(i, 8)].astype(F32).reshape(side, side)
+                loop(GROUP, widen)
+
+                def flip(i):
+                    for v in range(4):
+                        at = pl.ds(i * 4 + v, side, stride=GROUP)
+                        f_out[at] = f_in[at].T
+                loop(4, flip)
+
+                @pl.when(u >= 2)
+                def _():
+                    o_copy(u).wait()
+
+                def narrow(i):
+                    tout[u % 2, part(i, 8)] = f_out[part(i, side)].astype(BF).reshape(8, GROUP, side)
+                loop(GROUP, narrow)
+                o_copy(u).start()
+            loop(12, unit)
+            o_copy(10).wait()
+            o_copy(11).wait()
+
+        pl.run_scoped(
+            body, pltpu.VMEM((2, LANES, GROUP, LANES), BF), pltpu.VMEM((2, LANES, GROUP, LANES), BF),
+            pltpu.VMEM((LANES * GROUP, LANES), F32), pltpu.VMEM((LANES * GROUP, LANES), F32))
+
     def xb_copy(src):
         ref = b_all.at[:, rblk(src), lane(core)]
         return remote(ref, ref, xb_ssem.at[src], xb_rsem.at[src], sib)
@@ -371,6 +426,10 @@
         @pl.when(own_half == 1)
         def _():
             xa_copy(src // 2).start()
+
+        @pl.when(k == 3)
+        def _():
+            transpose(me // 4)
     loop(8, block)
 
     for k in range(1, 8):
@@ -391,7 +450,7 @@
         dst = rs_mid.at[ib] if t == 0 else rs_recv.at[t - 1, at]
         return remote(rt.at[t, at], dst, rs_ssem.at[n], rs_rsem.at[n], partner(me, k))
 
-    def contract(o_s, tm):
+    def contract(o_s):
         def outer(left, right_of):
             def qstep(qq):
                 for u in range(QSTEP):
@@ -435,14 +494,19 @@
                             rt[at] = (rt[at].astype(F32) + rs_mid[v - 4, i].astype(F32)).astype(BF)
                         loop(GROUP // 2, add)
                     rs_copy(v).start()
+                    if v == 0:
+                        for i in range(2):
+                            g_wait(i + 1).wait_recv()
+                            d_copy(i).start()
+                            f_copy(i).start()
                     if v == 1:
                         for k in (3, 5, 6, 7):
                             m_copy(k).start()
         loop(8, eblk)
 
-        for i in range(1, 4):
-            g_wait(i).wait_recv()
-            f_copy(i - 1).start()
+        for i in range(2):
+            d_wait(i).wait_recv()
+        f_copy(2).start()
         g_wait(0).wait_recv()
         for i in range(3):
             f_wait(i).wait_recv()
@@ -456,50 +520,44 @@
                     i = ii * RSTEP + u
                     row = ib * GROUP + i
                     r = jnp.dot(wo_m[:], o_s[i], preferred_element_type=F32)
-                    tm[row] = (r + bo_m[:]) / (NORM_EPS + cnt_m[row])
+                    pair_out[row] = ((r + bo_m[:]) / (NORM_EPS + cnt_m[row])).T
             loop(GROUP // RSTEP, rstep)
         loop(rows // GROUP, mblk)
 
-        def final(zb):
-            def z_copy(j):
-                return pltpu.make_async_copy(pair.at[pl.ds(j * 8, 8)], zb.at[j % 2], lsem.at[3 + j % 2])
-
-            def o_copy(j):
-                return pltpu.make_async_copy(zb.at[j % 2], pair_out.at[pl.ds(j * 8, 8)], lsem.at[5 + j % 2])
-
-            hi0 = lax.broadcasted_iota(jnp.int32, (LANES, LANES), 0) * 0 + chip // 2 == 0
-            odd = lax.broadcasted_iota(jnp.int32, (LANES, LANES), 0) * 0 + chip % 2 == 1
-            z_copy(0).start()
-            for j in range(rows // 8):
-                if j % 2 == 0:
-                    for n in ((2, 4), (3, 5))[j // 2]:
-                        rs_copy(n).wait_recv()
-                if j >= 1:
-                    o_copy(j - 1).wait()
-                if j + 1 < rows // 8:
-                    z_copy(j + 1).start()
-                z_copy(j).wait()
-
-                def row2(i):
-                    n = j * 4 + i
-                    tot = rt[3, n].astype(F32) + rs_recv[0, n].astype(F32) + rs_recv[1, n].astype(F32)
-                    kept, own = tot[:, 256:], r_own[n]
-                    rkept, rown = pltpu.roll(kept, HALF, 1), pltpu.roll(own, HALF, 1)
-                    near0 = jnp.where(lane_lo, jnp.where(odd, kept, own), jnp.where(odd, rown, rkept))
-                    near1 = jnp.where(lane_lo, jnp.where(odd, rkept, rown), jnp.where(odd, own, kept))
-                    for v, near in ((0, near0), (1, near1)):
-                        away = tot[:, v * LANES:v * LANES + LANES]
-                        row = n * 2 + v
-                        r = jnp.concatenate([jnp.where(hi0, near, away), jnp.where(hi0, away, near)], axis=1)
-                        te = (r + bo_e[:]) / (NORM_EPS + cnt_e[row])
-                        zb[j % 2, i * 2 + v] = (zb[j % 2, i * 2 + v] + te.T) + tm[row].T
-                loop(4, row2)
-                o_copy(j).start()
-            o_copy(rows // 8 - 1).wait()
-
-        pl.run_scoped(final, pltpu.VMEM((2, 8, res, LANES), F32))
-
-    pl.run_scoped(contract, pltpu.VMEM((GROUP, 1024, res), BF), pltpu.VMEM((rows, LANES, res), F32))
+    pl.run_scoped(contract, pltpu.VMEM((GROUP, 1024, res), BF))
+    transpose(1 - me // 4)
+
+    def final(zb):
+        def z_copy(j):
+            return pltpu.make_async_copy(pair.at[part(j, 8)], zb.at[part(j, 8)], lsem.at[3 + j])
+
+        steps = rows // 8
+        for j in range(steps):
+            z_copy(j).start()
+        hi0 = lax.broadcasted_iota(jnp.int32, (LANES, LANES), 0) * 0 + chip // 2 == 0
+        odd = lax.broadcasted_iota(jnp.int32, (LANES, LANES), 0) * 0 + chip % 2 == 1
+
+        def row2(n):
+            tot = rt[3, n].astype(F32) + rs_recv[0, n].astype(F32) + rs_recv[1, n].astype(F32)
+            kept, own = tot[:, 256:], r_own[n]
+            rkept, rown = pltpu.roll(kept, HALF, 1), pltpu.roll(own, HALF, 1)
+            near0 = jnp.where(lane_lo, jnp.where(odd, kept, own), jnp.where(odd, rown, rkept))
+            near1 = jnp.where(lane_lo, jnp.where(odd, rkept, rown), jnp.where(odd, own, kept))
+            for v, near in ((0, near0), (1, near1)):
+                away = tot[:, v * LANES:v * LANES + LANES]
+                row = n * 2 + v
+                r = jnp.concatenate([jnp.where(hi0, near, away), jnp.where(hi0, away, near)], axis=1)
+                te = (r + bo_e[:]) / (NORM_EPS + cnt_e[row])
+                pair_out[row] = (zb[row] + te.T) + pair_out[row]
+
+        for j in range(steps):
+            z_copy(j).wait()
+        for h in range(2):
+            for n in ((2, 4), (3, 5))[h]:
+                rs_copy(n).wait_recv()
+            loop(rows // 4, lambda i: row2(h * (rows // 4) + i))
+
+    pl.run_scoped(final, pltpu.VMEM((rows, res, LANES), F32))
 
     for k in range(1, 8):
         m_copy(k).wait_send()
@@ -513,8 +571,10 @@
     def drain_a(c):
         xa_copy(c).wait_send()
     loop(4, drain_a)
-    for i in range(4):
+    for i in range(3):
         g_copy(i).wait_send()
+    for i in range(2):
+        d_copy(i).wait_send()
     for i in range(3):
         f_copy(i).wait_send()
     for n in range(6):
@@ -541,14 +601,15 @@
         any_spec = pl.BlockSpec(memory_space=pl.ANY)
         vmem = pl.BlockSpec(memory_space=pltpu.VMEM)
         dma = pltpu.SemaphoreType.DMA
-        pair_out, e_recv, m_recv = pl.pallas_call(
+        pair_out, e_seq, m_seq, _ = pl.pallas_call(
             opm_kernel,
             out_shape=(
-                jax.ShapeDtypeStruct((rows, res, nk), F32),
-                jax.ShapeDtypeStruct((res, ce, seq), BF),
-                jax.ShapeDtypeStruct((mseqs // 8, res, cm), BF)),
+                pltpu.VMEM((rows, res, nk), F32),
+                jax.ShapeDtypeStruct((seq, ce, res), BF),
+                jax.ShapeDtypeStruct((mseqs // 8, res, cm), BF),
+                jax.ShapeDtypeStruct((res, ce, seq), BF)),
             in_specs=[any_spec, any_spec, any_spec, vmem, any_spec] + [vmem] * 16,
-            out_specs=(any_spec,) * 3,
+            out_specs=(vmem, any_spec, any_spec, any_spec),
             scratch_shapes=[
                 pltpu.VMEM((4 * rows * hid, 2 * seq), BF),
                 pltpu.VMEM((hid, res, 2 * seq), BF),
@@ -579,13 +640,14 @@
                 pltpu.VMEM((rows, 1, res), F32),
                 pltpu.VMEM((rows, 1, res), F32),
                 dma((8,)), dma((8,)), dma((8,)), dma((8,)), dma((4,)), dma((4,)), dma((8,)), dma((8,)),
-                dma((4,)), dma((4,)), dma((3,)), dma((3,)), dma((6,)), dma((6,)),
+                dma((2,)), dma((2,)), dma((2,)), dma((2,)),
+                dma((3,)), dma((3,)), dma((3,)), dma((3,)), dma((6,)), dma((6,)),
                 dma((8,)), dma((8,)), pltpu.SemaphoreType.REGULAR, dma((8,))],
             compiler_params=pltpu.CompilerParams(
-                collective_id=0, has_side_effects=True, vmem_limit_bytes=67043328),
+                collective_id=0, has_side_effects=True, vmem_limit_bytes=VMEM_LIMIT),
             name='opm',
         )(*args)
-        return pair_out, jnp.transpose(e_recv, (2, 0, 1)), m_recv
+        return pair_out, jnp.transpose(e_seq, (0, 2, 1)), m_seq
 
     in_specs = (msa_spec, mask_spec, msa_spec, mask_spec, row_spec) + (P(),) * 16
     return jax.shard_map(local_program, mesh=mesh, in_specs=in_specs, out_specs=(row_spec,) * 3, check_vma=False)

time: 298 us -> 290 us (0.973)
  local copies, waits for them, and re-layouts: 24.8 us -> 15 us
    unnamed x5, local copies, waits for them, and re-layouts: 24.8 us -> 15 us
where the time goes in v4:
time: 290 us; the launch traced here: 288 us
  Pallas kernels  272 us (94%)
  local copies, waits for them, and re-layouts  15 us (5%)
    pallas_call x1, Pallas kernels, local_program(): pl.pallas_call(opm_kernel, out_shape=(pltpu.VMEM((rows, res, nk), F32), j...  272 us
    unnamed x5, local copies, waits for them, and re-layouts  15 us

profile of v4, /device:TPU:0, one launch (start us, length us, event | category | flops | bytes accessed | tf_op | source)
XLA Modules:
  0.0 287.9 jit_solution(11235230601989737970)
XLA Ops:
  0.6 272.2 %opm.1 = (f32[32,256,128]{2,1,0:T(8,128)S(1)}, bf16[384,64,256]{2,1,0:T(8,128)(2,1)}, bf16[32,256,256]{2,1,0:T(8,128)(2,1)}, bf16[256,64,384]{2,1,0:T(8,128)(2,1)}) custom-call(bf16[32,64,3072]{2,1,0:T(8,128)(2,1)} %bitcast.6, bf16[256,32,256]{2,1,0:T(8,128)(2,1)} %xm.1, s32[3072,256]{1,0:T(8,128)} %mask_e.1, s32[256,256]{1,0:T(8,128)} %mask_m.1, ...), custom_call_target="tpu_custom_call" | custom-call | tf_op jit(solution)/shard_map/opm/pallas_call | solution.py:604
  272.8 2.0 copy.27
  274.8 0.0 copy-start
  274.8 11.0 %copy.28 = bf16[384,256,64]{1,2,0:T(8,128)(2,1)} copy(bf16[384,256,64]{1,2,0:T(8,128)(2,1)} %bitcast.7) | data formatting | bytes 25165824
  285.8 0.0 copy-done
  285.8 2.0 copy.29
Async XLA Ops:
  274.8 11.0 %copy-start = (bf16[32,256,256]{2,1,0:T(8,128)(2,1)S(1)}, bf16[32,256,256]{2,1,0:T(8,128)(2,1)}, u32[]{:S(2)}) copy-start(bf16[32,256,256]{2,1,0:T(8,128)(2,1)} %get-tuple-element.17) | copy-start | bytes 12582916

commit v5 on v4

--- a/solution.py
+++ b/solution.py
@@ -12,7 +12,7 @@
 BF = jnp.bfloat16
 F32 = jnp.float32
 GROUP = 16
-VMEM_LIMIT = 58 * 2 ** 20
+VMEM_LIMIT = 55 * 2 ** 20
 QSTEP = 4
 LSTEP = 4
 MSTEP = 8
@@ -152,9 +152,7 @@
         cp = pltpu.make_async_copy(xm.at[rblk(me, mseq)], xc.at[pl.ds(0, mseq)], lsem.at[1])
         cp.start()
         cp.wait()
-        cp = pltpu.make_async_copy(xc.at[pl.ds(0, mseq)], m_out.at[:, rblk(me), :], lsem.at[1])
-        cp.start()
-        cp.wait()
+        m_out[:, rblk(me), :] = xc[pl.ds(0, mseq)]
         step = xc.shape[0]
         gam_m, bet_m = row_of(m_gam), row_of(m_bet)
         for piece in range(xm.shape[0] // step):
@@ -450,37 +448,40 @@
         dst = rs_mid.at[ib] if t == 0 else rs_recv.at[t - 1, at]
         return remote(rt.at[t, at], dst, rs_ssem.at[n], rs_rsem.at[n], partner(me, k))
 
-    def contract(o_s):
-        def outer(left, right_of):
-            def qstep(qq):
-                for u in range(QSTEP):
-                    q = qq * QSTEP + u
-                    o = nt_dot(left(), right_of(q))
-                    o_s[:, part(q, HID), :] = o.astype(BF).reshape(GROUP, HID, res)
-            loop(HID // QSTEP, qstep)
+    def contract_extra(o_s):
+        pairs = GROUP // 2
+        low = lax.broadcasted_iota(jnp.int32, (pairs * HID, LANES), 1) < HALF
 
         def eblk(n):
             t = ((n // 2 + 1) // 2) % 2 * (1 + (n // 2 + n + 1) % 2) + 3 * (n // 6)
             ib = n % 2
             c = partner(me, 2 * (1 - t // 2) + 4 * (1 - t % 2)) // 2
             at = pl.ds(pl.multiple_of((c * rows + ib * GROUP) * HID, GROUP * HID), GROUP * HID)
-            outer(lambda: a_all[at, :], lambda q: b_all[q])
-
-            hi0 = lax.broadcasted_iota(jnp.int32, (LANES, LANES), 0) * 0 + c // 2 == 0
-            odd = lax.broadcasted_iota(jnp.int32, (LANES, LANES), 0) * 0 + c % 2 == 1
+            away_at = part(1 - c // 2, LANES)
+            near_at = part(c // 2 * 2 + 1 - c % 2, HALF)
+
+            def qstep(qq):
+                for h in range(2):
+                    q = qq * QSTEP + h * 2
+                    o = nt_dot(a_all[at, :], b_all[pl.ds(q, 2), away_at, :].reshape(256, 2 * seq))
+                    o = o.astype(BF).reshape(pairs, 2, HID, 256)
+                    for v in range(2):
+                        for x in range(2):
+                            o_s[:, part(q + x, HID), pl.ds(v * LANES, LANES)] = o[:, v, :, x * LANES:x * LANES + LANES]
+                q = qq * QSTEP
+                o = nt_dot(a_all[at, :], b_all[pl.ds(q, QSTEP), near_at, :].reshape(256, 2 * seq))
+                o = o.reshape(pairs, 2, HID, 256)
+                for x in range(2):
+                    u0, u1 = (o[:, v, :, x * LANES:x * LANES + LANES].reshape(pairs * HID, LANES) for v in range(2))
+                    for y, near in ((0, jnp.where(low, u0, pltpu.roll(u1, HALF, 1))),
+                                    (1, jnp.where(low, pltpu.roll(u0, HALF, 1), u1))):
+                        o_s[:, part(q + x * 2 + y, HID), pl.ds(2 * LANES, LANES)] = near.astype(BF).reshape(pairs, HID, LANES)
+            loop(HID // QSTEP, qstep)
 
             def rstep(ii):
                 for u in range(RSTEP // 2):
-                    n2 = ii * (RSTEP // 2) + u
-                    away, near = [], []
-                    for v in range(2):
-                        r = jnp.dot(wo_e[:], o_s[n2 * 2 + v], preferred_element_type=F32)
-                        away.append(jnp.where(hi0, r[:, LANES:], r[:, :LANES]))
-                        near.append(jnp.where(hi0, r[:, :LANES], r[:, LANES:]))
-                    n0 = jnp.where(odd, near[0], pltpu.roll(near[0], HALF, 1))
-                    n1 = jnp.where(odd, pltpu.roll(near[1], HALF, 1), near[1])
-                    rt[t, ib * (GROUP // 2) + n2] = jnp.concatenate(
-                        [away[0], away[1], jnp.where(lane_lo, n0, n1)], axis=1).astype(BF)
+                    i = ii * (RSTEP // 2) + u
+                    rt[t, ib * pairs + i] = jnp.dot(wo_e[:], o_s[i], preferred_element_type=F32).astype(BF)
             loop(GROUP // RSTEP, rstep)
 
             for v in range(6):
@@ -511,9 +512,15 @@
         for i in range(3):
             f_wait(i).wait_recv()
 
+    def contract_main(o_s):
         def mblk(ib):
             at = part(ib, GROUP * HID)
-            outer(lambda: am[at, :], lambda q: bm[q])
+
+            def qstep(qq):
+                for u in range(QSTEP):
+                    q = qq * QSTEP + u
+                    o_s[:, part(q, HID), :] = nt_dot(am[at, :], bm[q]).astype(BF).reshape(GROUP, HID, res)
+            loop(HID // QSTEP, qstep)
 
             def rstep(ii):
                 for u in range(RSTEP):
@@ -524,7 +531,8 @@
             loop(GROUP // RSTEP, rstep)
         loop(rows // GROUP, mblk)
 
-    pl.run_scoped(contract, pltpu.VMEM((GROUP, 1024, res), BF))
+    pl.run_scoped(contract_extra, pltpu.VMEM((GROUP // 2, 1024, 3 * LANES), BF))
+    pl.run_scoped(contract_main, pltpu.VMEM((GROUP, 1024, res), BF))
     transpose(1 - me // 4)
 
     def final(zb):
@@ -606,10 +614,10 @@
             out_shape=(
                 pltpu.VMEM((rows, res, nk), F32),
                 jax.ShapeDtypeStruct((seq, ce, res), BF),
-                jax.ShapeDtypeStruct((mseqs // 8, res, cm), BF),
+                pltpu.VMEM((mseqs // 8, res, cm), BF),
                 jax.ShapeDtypeStruct((res, ce, seq), BF)),
             in_specs=[any_spec, any_spec, any_spec, vmem, any_spec] + [vmem] * 16,
-            out_specs=(vmem, any_spec, any_spec, any_spec),
+            out_specs=(vmem, any_spec, vmem, any_spec),
             scratch_shapes=[
                 pltpu.VMEM((4 * rows * hid, 2 * seq), BF),
                 pltpu.VMEM((hid, res, 2 * seq), BF),

time: 290 us -> 278 us (0.959)
  Pallas kernels: 272 us -> 263 us
    pallas_call x1, Pallas kernels: 272 us -> 263 us  [local_program(): pl.pallas_call(opm_kernel, out_shape=(pltpu.VMEM((rows, res, nk), F32), j...]
where the time goes in v5:
time: 278 us; the launch traced here: 276 us
  Pallas kernels  263 us (95%)
  local copies, waits for them, and re-layouts  12.4 us (4%)
    pallas_call x1, Pallas kernels, local_program(): pl.pallas_call(opm_kernel, out_shape=(pltpu.VMEM((rows, res, nk), F32), j...  263 us
    unnamed x5, local copies, waits for them, and re-layouts  12.4 us

profile of v5, /device:TPU:0, one launch (start us, length us, event | category | flops | bytes accessed | tf_op | source)
XLA Modules:
  0.0 276.4 jit_solution(13681370934883380903)
XLA Ops:
  0.6 263.4 %opm.1 = (f32[32,256,128]{2,1,0:T(8,128)S(1)}, bf16[384,64,256]{2,1,0:T(8,128)(2,1)}, bf16[32,256,256]{2,1,0:T(8,128)(2,1)S(1)}, bf16[256,64,384]{2,1,0:T(8,128)(2,1)}) custom-call(bf16[32,64,3072]{2,1,0:T(8,128)(2,1)} %bitcast.6, bf16[256,32,256]{2,1,0:T(8,128)(2,1)} %xm.1, s32[3072,256]{1,0:T(8,128)} %mask_e.1, s32[256,256]{1,0:T(8,128)} %mask_m.1, ...), custom_call_target="tpu_custom_call" | custom-call | tf_op jit(solution)/shard_map/opm/pallas_call | solution.py:612
  264.0 0.0 copy-start
  264.1 2.1 copy.27
  266.2 2.1 copy.28
  268.3 3.3 %copy-done = bf16[384,64,256]{2,1,0:T(8,128)(2,1)S(1)} copy-done((bf16[384,64,256]{2,1,0:T(8,128)(2,1)S(1)}, bf16[384,64,256]{2,1,0:T(8,128)(2,1)}, u32[]{:S(2)}) %copy-start) | copy-done | bytes 12582936
  271.6 4.8 %copy.29 = bf16[384,256,64]{1,2,0:T(8,128)(2,1)} copy(bf16[384,256,64]{1,2,0:T(8,128)(2,1)S(1)} %bitcast.7) | data formatting | bytes 25165824
Async XLA Ops:
  264.0 7.6 %copy-start = (bf16[384,64,256]{2,1,0:T(8,128)(2,1)S(1)}, bf16[384,64,256]{2,1,0:T(8,128)(2,1)}, u32[]{:S(2)}) copy-start(bf16[384,64,256]{2,1,0:T(8,128)(2,1)} %get-tuple-element.7) | copy-start | bytes 37748740

commit v6 on v5

--- a/solution.py
+++ b/solution.py
@@ -12,7 +12,7 @@
 BF = jnp.bfloat16
 F32 = jnp.float32
 GROUP = 16
-VMEM_LIMIT = 55 * 2 ** 20
+VMEM_LIMIT = 43 * 2 ** 20
 QSTEP = 4
 LSTEP = 4
 MSTEP = 8
@@ -53,10 +53,10 @@
     e_gam, e_bet, e_wl, e_bl, e_wr, e_br, e_wo, e_bo,
     m_gam, m_bet, m_wl, m_bl, m_wr, m_br, m_wo, m_bo,
     pair_out, e_t, m_out, e_out,
-    a_all, b_all, a_send, xb, y_s, mask_i, mask_et, mask_mo, am, bm, rt, rs_mid, rs_recv, r_own,
+    a_all, a_send, xb, y_s, mask_i, mask_et, mask_mo, am, bm, rt, rs_mid, rs_recv, r_own,
     w_right, w_left, w_m, wo_e, wo_m, gam_e, bet_e, bias_b, bias_a, bo_e, bias_m, bo_m, cnt_e, cnt_m,
     e_ssem, e_rsem, m_ssem, m_rsem, xa_ssem, xa_rsem, xb_ssem, xb_rsem,
-    d_ssem, d_rsem, t_isem, t_osem, g_ssem, g_rsem, f_ssem, f_rsem, rs_ssem, rs_rsem, ob_ssem, ob_rsem, ob_free, lsem,
+    d_ssem, d_rsem, t_isem, g_ssem, g_rsem, f_ssem, f_rsem, rs_ssem, rs_rsem, ob_ssem, ob_rsem, ob_free, lsem,
 ):
     me = lax.axis_index('dap')
     core = me % 2
@@ -323,67 +323,51 @@
         own_pairs, pltpu.VMEM((res, seq), F32), pltpu.VMEM((rows, res), F32),
         pltpu.VMEM((2, rows * HID, seq), BF), pltpu.VMEM((8, rows * HID, 256), F32), pltpu.VMEM((1024, LANES), BF))
 
-    def transpose(yh):
-        def body(tin, tout, f_in, f_out):
-            side = GROUP * 8
-
-            def i_copy(u):
-                return pltpu.make_async_copy(
-                    e_out.at[part(yh, side), part(u % 4, GROUP), part(u // 4, side)], tin.at[u % 2], t_isem.at[u % 2])
-
-            def o_copy(u):
-                return pltpu.make_async_copy(
-                    tout.at[u % 2], e_t.at[part(u // 4, side), part(u % 4, GROUP), part(yh, side)], t_osem.at[u % 2])
-
-            i_copy(0).start()
-
-            def unit(u):
-                @pl.when(u < 11)
-                def _():
-                    i_copy(u + 1).start()
-                i_copy(u).wait()
-
-                def widen(i):
-                    f_in[part(i, side)] = tin[u % 2, part(i, 8)].astype(F32).reshape(side, side)
-                loop(GROUP, widen)
-
-                def flip(i):
-                    for v in range(4):
-                        at = pl.ds(i * 4 + v, side, stride=GROUP)
-                        f_out[at] = f_in[at].T
-                loop(4, flip)
-
-                @pl.when(u >= 2)
-                def _():
-                    o_copy(u).wait()
-
-                def narrow(i):
-                    tout[u % 2, part(i, 8)] = f_out[part(i, side)].astype(BF).reshape(8, GROUP, side)
-                loop(GROUP, narrow)
-                o_copy(u).start()
-            loop(12, unit)
-            o_copy(10).wait()
-            o_copy(11).wait()
-
-        pl.run_scoped(
-            body, pltpu.VMEM((2, LANES, GROUP, LANES), BF), pltpu.VMEM((2, LANES, GROUP, LANES), BF),
-            pltpu.VMEM((LANES * GROUP, LANES), F32), pltpu.VMEM((LANES * GROUP, LANES), F32))
-
-    def xb_copy(src):
-        ref = b_all.at[:, rblk(src), lane(core)]
-        return remote(ref, ref, xb_ssem.at[src], xb_rsem.at[src], sib)
-
-    def xb_wait(src):
-        ref = b_all.at[:, rblk(src), lane(1 - core)]
-        return remote(ref, ref, xb_ssem.at[src], xb_rsem.at[src], sib)
-
-    def xa_copy(c):
-        return remote(a_send.at[rblk(c, rows * HID)], a_all.at[rblk(c, rows * HID), lane(core)],
-                      xa_ssem.at[c], xa_rsem.at[c], sib)
-
-    def xa_wait(c):
-        return remote(a_send.at[rblk(c, rows * HID)], a_all.at[rblk(c, rows * HID), lane(1 - core)],
-                      xa_ssem.at[c], xa_rsem.at[c], sib)
+    def transpose(tin, f_in, f_out):
+        side = GROUP * 8
+        units = 24
+
+        def i_copy(u):
+            return pltpu.make_async_copy(
+                e_out.at[part(u // 12, side), part(u % 4, GROUP), part(u // 4 % 3, side)], tin.at[u % 2], t_isem.at[u % 2])
+
+        i_copy(0).start()
+
+        def unit(u):
+            @pl.when(u < units - 1)
+            def _():
+                i_copy(u + 1).start()
+            i_copy(u).wait()
+
+            def widen(i):
+                f_in[part(i, side)] = tin[u % 2, part(i, 8)].astype(F32).reshape(side, side)
+            loop(GROUP, widen)
+
+            def flip(i):
+                for v in range(4):
+                    at = pl.ds(i * 4 + v, side, stride=GROUP)
+                    f_out[at] = f_in[at].T
+            loop(4, flip)
+
+            def narrow(i):
+                e_t[part(u // 4 % 3 * GROUP + i, 8), part(u % 4, GROUP), part(u // 12, side)] = (
+                    f_out[part(i, side)].astype(BF).reshape(8, GROUP, side))
+            loop(GROUP, narrow)
+        loop(units, unit)
+
+    def b_rows(kk, c):
+        return part(kk * 4 + c, HID)
+
+    def k_lane(kk, h):
+        return pl.ds(pl.multiple_of(kk * 256 + h * LANES, LANES), LANES)
+
+    def xb_copy(src, kk, h):
+        ref = e_t.at[b_rows(kk, src // 2), part(src % 2, rows), part(h, LANES)]
+        return remote(ref, ref, xb_ssem.at[src, kk], xb_rsem.at[src, kk], sib)
+
+    def xa_copy(c, kk, h):
+        return remote(a_send.at[rblk(c, rows * HID), pl.ds(kk * LANES, LANES)], a_all.at[rblk(c, rows * HID), k_lane(kk, h)],
+                      xa_ssem.at[c, kk], xa_rsem.at[c, kk], sib)
 
     def block(k):
         src = partner(me, k)
@@ -408,26 +392,27 @@
         def half(hh):
             r0 = pl.multiple_of(src * rows + hh * GROUP, GROUP)
             right, left = project(hh, mask_et[pl.ds(r0, GROUP), :])
-            b_all[:, pl.ds(r0, GROUP), lane(core)] = right
+            for kk in range(3):
+                r_at = pl.ds(pl.multiple_of(src % 2 * rows + hh * GROUP, GROUP), GROUP)
+                e_t[b_rows(kk, src // 2), r_at, part(core, LANES)] = right[:, :, kk * LANES:kk * LANES + LANES]
             at = pl.ds(pl.multiple_of(((src // 2) * rows + hh * GROUP) * HID, GROUP * HID), GROUP * HID)
 
             @pl.when(own_half == 0)
             def _():
-                a_all[at, lane(core)] = left
+                for kk in range(3):
+                    a_all[at, k_lane(kk, core)] = left[:, kk * LANES:kk * LANES + LANES]
 
             @pl.when(own_half == 1)
             def _():
                 a_send[at, :] = left
         loop(rows // GROUP, half)
-        xb_copy(src).start()
+        for kk in range(3):
+            xb_copy(src, kk, core).start()
 
         @pl.when(own_half == 1)
         def _():
-            xa_copy(src // 2).start()
-
-        @pl.when(k == 3)
-        def _():
-            transpose(me // 4)
+            for kk in range(3):
+                xa_copy(src // 2, kk, core).start()
     loop(8, block)
 
     for k in range(1, 8):
@@ -435,17 +420,20 @@
 
 
     def xwait(s):
-        xb_wait(s).wait_recv()
+        for kk in range(3):
+            xb_copy(s, kk, 1 - core).wait_recv()
     loop(8, xwait)
 
     def xwait_a(c):
-        xa_wait(c).wait_recv()
+        for kk in range(3):
+            xa_copy(c, kk, 1 - core).wait_recv()
     loop(4, xwait_a)
 
     def rs_copy(n):
-        t, ib, k = ((0, 0, 2), (0, 1, 4), (1, 0, 2), (2, 1, 4), (2, 0, 4), (1, 1, 2))[n]
-        at = pl.ds(ib * GROUP // 2, GROUP // 2)
-        dst = rs_mid.at[ib] if t == 0 else rs_recv.at[t - 1, at]
+        t, first, count, k = ((0, 0, 8, 2), (0, 8, 8, 4), (1, 0, 8, 2), (2, 8, 8, 4),
+                              (2, 0, 4, 4), (1, 8, 4, 2), (2, 4, 4, 4), (1, 12, 4, 2))[n]
+        at = pl.ds(first, count)
+        dst = rs_mid.at[first // 8] if t == 0 else rs_recv.at[t - 1, at]
         return remote(rt.at[t, at], dst, rs_ssem.at[n], rs_rsem.at[n], partner(me, k))
 
     def contract_extra(o_s):
@@ -457,25 +445,29 @@
             ib = n % 2
             c = partner(me, 2 * (1 - t // 2) + 4 * (1 - t % 2)) // 2
             at = pl.ds(pl.multiple_of((c * rows + ib * GROUP) * HID, GROUP * HID), GROUP * HID)
-            away_at = part(1 - c // 2, LANES)
-            near_at = part(c // 2 * 2 + 1 - c % 2, HALF)
+            away = (1 - c // 2) * 2
+            near = c // 2 * 2 + 1 - c % 2
+
+            def right(blocks):
+                return jnp.concatenate([jnp.concatenate(
+                    [e_t[(kk * 4 + chip_j) * HID + q] for q, chip_j in blocks], axis=0) for kk in range(3)], axis=1)
 
             def qstep(qq):
                 for h in range(2):
                     q = qq * QSTEP + h * 2
-                    o = nt_dot(a_all[at, :], b_all[pl.ds(q, 2), away_at, :].reshape(256, 2 * seq))
+                    o = nt_dot(a_all[at, :], right([(q + x, away + y) for x in range(2) for y in range(2)]))
                     o = o.astype(BF).reshape(pairs, 2, HID, 256)
                     for v in range(2):
                         for x in range(2):
                             o_s[:, part(q + x, HID), pl.ds(v * LANES, LANES)] = o[:, v, :, x * LANES:x * LANES + LANES]
                 q = qq * QSTEP
-                o = nt_dot(a_all[at, :], b_all[pl.ds(q, QSTEP), near_at, :].reshape(256, 2 * seq))
+                o = nt_dot(a_all[at, :], right([(q + x, near) for x in range(QSTEP)]))
                 o = o.reshape(pairs, 2, HID, 256)
                 for x in range(2):
                     u0, u1 = (o[:, v, :, x * LANES:x * LANES + LANES].reshape(pairs * HID, LANES) for v in range(2))
-                    for y, near in ((0, jnp.where(low, u0, pltpu.roll(u1, HALF, 1))),
+                    for y, both in ((0, jnp.where(low, u0, pltpu.roll(u1, HALF, 1))),
                                     (1, jnp.where(low, pltpu.roll(u0, HALF, 1), u1))):
-                        o_s[:, part(q + x * 2 + y, HID), pl.ds(2 * LANES, LANES)] = near.astype(BF).reshape(pairs, HID, LANES)
+                        o_s[:, part(q + x * 2 + y, HID), pl.ds(2 * LANES, LANES)] = both.astype(BF).reshape(pairs, HID, LANES)
             loop(HID // QSTEP, qstep)
 
             def rstep(ii):
@@ -489,12 +481,15 @@
                 def _():
                     if v >= 4:
                         rs_copy(v - 4).wait_recv()
-
-                        def add(i):
-                            at = (t, ib * (GROUP // 2) + i)
-                            rt[at] = (rt[at].astype(F32) + rs_mid[v - 4, i].astype(F32)).astype(BF)
-                        loop(GROUP // 2, add)
-                    rs_copy(v).start()
+                        for h in range(2):
+                            def add(i):
+                                i = h * 4 + i
+                                at = (t, ib * pairs + i)
+                                rt[at] = (rt[at].astype(F32) + rs_mid[v - 4, i].astype(F32)).astype(BF)
+                            loop(4, add)
+                            rs_copy(v + h * 2).start()
+                    else:
+                        rs_copy(v).start()
                     if v == 0:
                         for i in range(2):
                             g_wait(i + 1).wait_recv()
@@ -533,7 +528,19 @@
 
     pl.run_scoped(contract_extra, pltpu.VMEM((GROUP // 2, 1024, 3 * LANES), BF))
     pl.run_scoped(contract_main, pltpu.VMEM((GROUP, 1024, res), BF))
-    transpose(1 - me // 4)
+    def drain(s):
+        for kk in range(3):
+            xb_copy(s, kk, core).wait_send()
+    loop(8, drain)
+
+    def drain_a(c):
+        for kk in range(3):
+            xa_copy(c, kk, core).wait_send()
+    loop(4, drain_a)
+
+    pl.run_scoped(
+        transpose, pltpu.VMEM((2, LANES, GROUP, LANES), BF), pltpu.VMEM((LANES * GROUP, LANES), F32),
+        pltpu.VMEM((LANES * GROUP, LANES), F32))
 
     def final(zb):
         def z_copy(j):
@@ -560,10 +567,10 @@
 
         for j in range(steps):
             z_copy(j).wait()
-        for h in range(2):
-            for n in ((2, 4), (3, 5))[h]:
+        for first, parts in ((0, (2, 4)), (8, (3, 5)), (4, (6,)), (12, (7,))):
+            for n in parts:
                 rs_copy(n).wait_recv()
-            loop(rows // 4, lambda i: row2(h * (rows // 4) + i))
+            loop(4, lambda i: row2(first + i))
 
     pl.run_scoped(final, pltpu.VMEM((rows, res, LANES), F32))
 
@@ -572,21 +579,24 @@
         to = partner(me, k)
         remote(xm.at[rblk(me, mseq)], m_out.at[:, rblk(to), :], m_ssem.at[k], m_rsem.at[k], to).wait_recv()
 
-    def drain(s):
-        xb_copy(s).wait_send()
-    loop(8, drain)
-
-    def drain_a(c):
-        xa_copy(c).wait_send()
-    loop(4, drain_a)
     for i in range(3):
         g_copy(i).wait_send()
     for i in range(2):
         d_copy(i).wait_send()
     for i in range(3):
         f_copy(i).wait_send()
-    for n in range(6):
+    for n in range(8):
         rs_copy(n).wait_send()
+
+
+def store_kernel(pair_in, e_in, m_in, pair_out, e_out, m_out, sem):
+    copies = []
+    for i, (src, dst) in enumerate(((pair_in, pair_out), (e_in, e_out), (m_in, m_out))):
+        copies.append(pltpu.make_async_copy(src, dst, sem.at[i]))
+    for copy in copies:
+        copy.start()
+    for copy in copies:
+        copy.wait()
 
 
 def solution(mesh):
@@ -613,14 +623,13 @@
             opm_kernel,
             out_shape=(
                 pltpu.VMEM((rows, res, nk), F32),
-                jax.ShapeDtypeStruct((seq, ce, res), BF),
+                pltpu.VMEM((seq, ce, res), BF),
                 pltpu.VMEM((mseqs // 8, res, cm), BF),
                 jax.ShapeDtypeStruct((res, ce, seq), BF)),
             in_specs=[any_spec, any_spec, any_spec, vmem, any_spec] + [vmem] * 16,
-            out_specs=(vmem, any_spec, vmem, any_spec),
+            out_specs=(vmem, vmem, vmem, any_spec),
             scratch_shapes=[
                 pltpu.VMEM((4 * rows * hid, 2 * seq), BF),
-                pltpu.VMEM((hid, res, 2 * seq), BF),
                 pltpu.VMEM((4 * rows * hid, seq), BF),
                 pltpu.VMEM((rows, ce, seq), BF),
                 pltpu.VMEM((GROUP * ce, seq), BF),
@@ -647,14 +656,23 @@
                 pltpu.VMEM((nk, 1), F32),
                 pltpu.VMEM((rows, 1, res), F32),
                 pltpu.VMEM((rows, 1, res), F32),
-                dma((8,)), dma((8,)), dma((8,)), dma((8,)), dma((4,)), dma((4,)), dma((8,)), dma((8,)),
-                dma((2,)), dma((2,)), dma((2,)), dma((2,)),
-                dma((3,)), dma((3,)), dma((3,)), dma((3,)), dma((6,)), dma((6,)),
+                dma((8,)), dma((8,)), dma((8,)), dma((8,)), dma((4, 3)), dma((4, 3)), dma((8, 3)), dma((8, 3)),
+                dma((2,)), dma((2,)), dma((2,)),
+                dma((3,)), dma((3,)), dma((3,)), dma((3,)), dma((8,)), dma((8,)),
                 dma((8,)), dma((8,)), pltpu.SemaphoreType.REGULAR, dma((8,))],
             compiler_params=pltpu.CompilerParams(
                 collective_id=0, has_side_effects=True, vmem_limit_bytes=VMEM_LIMIT),
             name='opm',
         )(*args)
+        pair_out, e_seq, m_seq = pl.pallas_call(
+            store_kernel,
+            out_shape=tuple(jax.ShapeDtypeStruct(x.shape, x.dtype) for x in (pair_out, e_seq, m_seq)),
+            in_specs=[vmem] * 3,
+            out_specs=(any_spec,) * 3,
+            scratch_shapes=[dma((3,))],
+            compiler_params=pltpu.CompilerParams(vmem_limit_bytes=2 ** 20),
+            name='store',
+        )(pair_out, e_seq, m_seq)
         return pair_out, jnp.transpose(e_seq, (0, 2, 1)), m_seq
 
     in_specs = (msa_spec, mask_spec, msa_spec, mask_spec, row_spec) + (P(),) * 16

time: 278 us -> 282 us (1.014)
  Pallas kernels: 263 us -> 279 us
  local copies, waits for them, and re-layouts: 12.4 us -> 0 us
    pallas_call x1 -> x2, Pallas kernels: 263 us -> 279 us  [the longest x1 272 us: local_program(): pl.pallas_call(opm_kernel, out_shape=(pltpu.VMEM((rows, res, nk), F32), p...]
    unnamed x5 -> x0, local copies, waits for them, and re-layouts: 12.4 us -> none
where the time goes in v6:
time: 282 us; the launch traced here: 280 us
  Pallas kernels  279 us (99%)
    pallas_call x1, Pallas kernels, local_program(): pl.pallas_call(opm_kernel, out_shape=(pltpu.VMEM((rows, res, nk), F32), p...  272 us
    pallas_call x1, Pallas kernels, local_program(): pl.pallas_call(store_kernel, out_shape=tuple((jax.ShapeDtypeStruct(x.shap...  7.21 us

profile of v6, /device:TPU:0, one launch (start us, length us, event | category | flops | bytes accessed | tf_op | source)
XLA Modules:
  0.0 280.0 jit_solution(9903870540443854293)
XLA Ops:
  0.6 272.1 %opm.1 = (f32[32,256,128]{2,1,0:T(8,128)S(1)}, bf16[384,64,256]{2,1,0:T(8,128)(2,1)S(1)}, bf16[32,256,256]{2,1,0:T(8,128)(2,1)S(1)}, bf16[256,64,384]{2,1,0:T(8,128)(2,1)}) custom-call(bf16[32,64,3072]{2,1,0:T(8,128)(2,1)} %bitcast.6, bf16[256,32,256]{2,1,0:T(8,128)(2,1)} %xm.1, s32[3072,256]{1,0:T(8,128)} %mask_e.1, s32[256,256]{1,0:T(8,128)} %mask_m.1, ...), custom_call_target="tpu_custom_call" | custom-call | tf_op jit(solution)/shard_map/opm/pallas_call | solution.py:622
  272.8 7.2 %store.1 = (f32[32,256,128]{2,1,0:T(8,128)}, bf16[384,64,256]{2,1,0:T(8,128)(2,1)}, bf16[32,256,256]{2,1,0:T(8,128)(2,1)}) custom-call(f32[32,256,128]{2,1,0:T(8,128)S(1)} %get-tuple-element.9.pair_in, bf16[384,64,256]{2,1,0:T(8,128)(2,1)S(1)} %get-tuple-element.10.e_in, bf16[32,256,256]{2,1,0:T(8,128)(2,1)S(1)} %get-tuple-element.11.m_in), custom_call_target="tpu_custom_call" | custom-call | tf_op jit(solution)/shard_map/store/pallas_call | solution.py:667

commit v7 on v6

--- a/solution.py
+++ b/solution.py
@@ -52,11 +52,11 @@
     xe, xm, mask_e, mask_m, pair,
     e_gam, e_bet, e_wl, e_bl, e_wr, e_br, e_wo, e_bo,
     m_gam, m_bet, m_wl, m_bl, m_wr, m_br, m_wo, m_bo,
-    pair_out, e_t, m_out, e_out,
+    pair_out, e_t, m_out, e_out, e_half,
     a_all, a_send, xb, y_s, mask_i, mask_et, mask_mo, am, bm, rt, rs_mid, rs_recv, r_own,
     w_right, w_left, w_m, wo_e, wo_m, gam_e, bet_e, bias_b, bias_a, bo_e, bias_m, bo_m, cnt_e, cnt_m,
     e_ssem, e_rsem, m_ssem, m_rsem, xa_ssem, xa_rsem, xb_ssem, xb_rsem,
-    d_ssem, d_rsem, t_isem, g_ssem, g_rsem, f_ssem, f_rsem, rs_ssem, rs_rsem, ob_ssem, ob_rsem, ob_free, lsem,
+    d_ssem, d_rsem, t_isem, t_osem, g_ssem, g_rsem, f_ssem, f_rsem, rs_ssem, rs_rsem, ob_ssem, ob_rsem, ob_free, lsem,
 ):
     me = lax.axis_index('dap')
     core = me % 2
@@ -323,13 +323,13 @@
         own_pairs, pltpu.VMEM((res, seq), F32), pltpu.VMEM((rows, res), F32),
         pltpu.VMEM((2, rows * HID, seq), BF), pltpu.VMEM((8, rows * HID, 256), F32), pltpu.VMEM((1024, LANES), BF))
 
-    def transpose(tin, f_in, f_out):
-        side = GROUP * 8
-        units = 24
-
+    side = GROUP * 8
+    units = 12
+
+    def transpose(yh, narrow, stored, tin, f_in, f_out):
         def i_copy(u):
             return pltpu.make_async_copy(
-                e_out.at[part(u // 12, side), part(u % 4, GROUP), part(u // 4 % 3, side)], tin.at[u % 2], t_isem.at[u % 2])
+                e_out.at[part(yh, side), part(u % 4, GROUP), part(u // 4, side)], tin.at[u % 2], t_isem.at[u % 2])
 
         i_copy(0).start()
 
@@ -348,12 +348,41 @@
                     at = pl.ds(i * 4 + v, side, stride=GROUP)
                     f_out[at] = f_in[at].T
             loop(4, flip)
-
-            def narrow(i):
-                e_t[part(u // 4 % 3 * GROUP + i, 8), part(u % 4, GROUP), part(u // 12, side)] = (
-                    f_out[part(i, side)].astype(BF).reshape(8, GROUP, side))
-            loop(GROUP, narrow)
+            stored(u)
+            loop(GROUP, lambda i: narrow(u, i, f_out[part(i, side)].astype(BF).reshape(8, GROUP, side)))
         loop(units, unit)
+
+    def early_half(tout, tin, f_in, f_out):
+        def o_copy(u):
+            return pltpu.make_async_copy(
+                tout.at[u % 2], e_half.at[part(u // 4, side), part(u % 4, GROUP), :], t_osem.at[u % 2])
+
+        def narrow(u, i, value):
+            tout[u % 2, part(i, 8)] = value
+
+            @pl.when(i == GROUP - 1)
+            def _():
+                o_copy(u).start()
+
+        def stored(u):
+            @pl.when(u >= 2)
+            def _():
+                o_copy(u).wait()
+
+        transpose(me // 4, narrow, stored, tin, f_in, f_out)
+        o_copy(units - 2).wait()
+        o_copy(units - 1).wait()
+
+    def late_half(tin, f_in, f_out):
+        yh = 1 - me // 4
+
+        def narrow(u, i, value):
+            e_t[part(u // 4 * GROUP + i, 8), part(u % 4, GROUP), part(yh, side)] = value
+
+        transpose(yh, narrow, lambda u: None, tin, f_in, f_out)
+
+    tile = pltpu.VMEM((2, LANES, GROUP, LANES), BF)
+    wide_tile = pltpu.VMEM((LANES * GROUP, LANES), F32)
 
     def b_rows(kk, c):
         return part(kk * 4 + c, HID)
@@ -413,6 +442,10 @@
         def _():
             for kk in range(3):
                 xa_copy(src // 2, kk, core).start()
+
+        @pl.when(k == 3)
+        def _():
+            pl.run_scoped(early_half, tile, tile, wide_tile, wide_tile)
     loop(8, block)
 
     for k in range(1, 8):
@@ -527,7 +560,6 @@
         loop(rows // GROUP, mblk)
 
     pl.run_scoped(contract_extra, pltpu.VMEM((GROUP // 2, 1024, 3 * LANES), BF))
-    pl.run_scoped(contract_main, pltpu.VMEM((GROUP, 1024, res), BF))
     def drain(s):
         for kk in range(3):
             xb_copy(s, kk, core).wait_send()
@@ -537,10 +569,11 @@
         for kk in range(3):
             xa_copy(c, kk, core).wait_send()
     loop(4, drain_a)
-
-    pl.run_scoped(
-        transpose, pltpu.VMEM((2, LANES, GROUP, LANES), BF), pltpu.VMEM((LANES * GROUP, LANES), F32),
-        pltpu.VMEM((LANES * GROUP, LANES), F32))
+    half_copy = pltpu.make_async_copy(e_half, e_t.at[:, :, part(me // 4, side)], lsem.at[2])
+    half_copy.start()
+    pl.run_scoped(contract_main, pltpu.VMEM((GROUP, 1024, res), BF))
+    pl.run_scoped(late_half, tile, wide_tile, wide_tile)
+    half_copy.wait()
 
     def final(zb):
         def z_copy(j):
@@ -619,15 +652,16 @@
         any_spec = pl.BlockSpec(memory_space=pl.ANY)
         vmem = pl.BlockSpec(memory_space=pltpu.VMEM)
         dma = pltpu.SemaphoreType.DMA
-        pair_out, e_seq, m_seq, _ = pl.pallas_call(
+        pair_out, e_seq, m_seq, _, _ = pl.pallas_call(
             opm_kernel,
             out_shape=(
                 pltpu.VMEM((rows, res, nk), F32),
                 pltpu.VMEM((seq, ce, res), BF),
                 pltpu.VMEM((mseqs // 8, res, cm), BF),
-                jax.ShapeDtypeStruct((res, ce, seq), BF)),
+                jax.ShapeDtypeStruct((res, ce, seq), BF),
+                jax.ShapeDtypeStruct((seq, ce, res // 2), BF)),
             in_specs=[any_spec, any_spec, any_spec, vmem, any_spec] + [vmem] * 16,
-            out_specs=(vmem, vmem, vmem, any_spec),
+            out_specs=(vmem, vmem, vmem, any_spec, any_spec),
             scratch_shapes=[
                 pltpu.VMEM((4 * rows * hid, 2 * seq), BF),
                 pltpu.VMEM((4 * rows * hid, seq), BF),
@@ -657,7 +691,7 @@
                 pltpu.VMEM((rows, 1, res), F32),
                 pltpu.VMEM((rows, 1, res), F32),
                 dma((8,)), dma((8,)), dma((8,)), dma((8,)), dma((4, 3)), dma((4, 3)), dma((8, 3)), dma((8, 3)),
-                dma((2,)), dma((2,)), dma((2,)),
+                dma((2,)), dma((2,)), dma((2,)), dma((2,)),
                 dma((3,)), dma((3,)), dma((3,)), dma((3,)), dma((8,)), dma((8,)),
                 dma((8,)), dma((8,)), pltpu.SemaphoreType.REGULAR, dma((8,))],
             compiler_params=pltpu.CompilerParams(

time: 282 us -> 271 us (0.961)
  Pallas kernels: 279 us -> 269 us
    pallas_call x1, Pallas kernels: 272 us -> 262 us  [local_program(): pl.pallas_call(opm_kernel, out_shape=(pltpu.VMEM((rows, res, nk), F32), p...]
where the time goes in v7:
time: 271 us; the launch traced here: 270 us
  Pallas kernels  269 us (99%)
    pallas_call x1, Pallas kernels, local_program(): pl.pallas_call(opm_kernel, out_shape=(pltpu.VMEM((rows, res, nk), F32), p...  262 us
    pallas_call x1, Pallas kernels, local_program(): pl.pallas_call(store_kernel, out_shape=tuple((jax.ShapeDtypeStruct(x.shap...  7.21 us

profile of v7, /device:TPU:0, one launch (start us, length us, event | category | flops | bytes accessed | tf_op | source)
XLA Modules:
  0.0 269.9 jit_solution(9083670304832078111)
XLA Ops:
  0.6 262.0 %opm.1 = (f32[32,256,128]{2,1,0:T(8,128)S(1)}, bf16[384,64,256]{2,1,0:T(8,128)(2,1)S(1)}, bf16[32,256,256]{2,1,0:T(8,128)(2,1)S(1)}, bf16[256,64,384]{2,1,0:T(8,128)(2,1)}, bf16[384,64,128]{2,1,0:T(8,128)(2,1)}) custom-call(bf16[32,64,3072]{2,1,0:T(8,128)(2,1)} %bitcast.6, bf16[256,32,256]{2,1,0:T(8,128)(2,1)} %xm.1, s32[3072,256]{1,0:T(8,128)} %mask_e.1, ...), custom_call_target="tpu_custom_call" | custom-call | tf_op jit(solution)/shard_map/opm/pallas_call | solution.py:655
  262.7 7.2 %store.1 = (f32[32,256,128]{2,1,0:T(8,128)}, bf16[384,64,256]{2,1,0:T(8,128)(2,1)}, bf16[32,256,256]{2,1,0:T(8,128)(2,1)}) custom-call(f32[32,256,128]{2,1,0:T(8,128)S(1)} %get-tuple-element.9.pair_in, bf16[384,64,256]{2,1,0:T(8,128)(2,1)S(1)} %get-tuple-element.10.e_in, bf16[32,256,256]{2,1,0:T(8,128)(2,1)S(1)} %get-tuple-element.11.m_in), custom_call_target="tpu_custom_call" | custom-call | tf_op jit(solution)/shard_map/store/pallas_call | solution.py:701

commit v8 on v7

--- a/solution.py
+++ b/solution.py
@@ -11,6 +11,7 @@
 NORM_EPS = 1e-3
 BF = jnp.bfloat16
 F32 = jnp.float32
+SMALL = 17
 GROUP = 16
 VMEM_LIMIT = 43 * 2 ** 20
 QSTEP = 4
@@ -48,8 +49,15 @@
     return jnp.sum(jnp.where(at == lax.broadcasted_iota(jnp.int32, (n, m), 1), row, 0.0), axis=1, keepdims=True)
 
 
-def opm_kernel(
-    xe, xm, mask_e, mask_m, pair,
+def opm_kernel(xe, xm, mask_e, pair, *refs):
+    raw, outs, small, scratch = refs[:SMALL], refs[SMALL:SMALL + 5], refs[SMALL + 5:SMALL * 2 + 5], refs[SMALL * 2 + 5:]
+    sems = scratch[-1]
+    copies = [pltpu.make_async_copy(src, dst, sems.at[i]) for i, (src, dst) in enumerate(zip(raw, small))]
+    opm_body(copies, xe, xm, mask_e, small[0], pair, *small[1:], *outs, *scratch[:-1])
+
+
+def opm_body(
+    copies, xe, xm, mask_e, mask_m, pair,
     e_gam, e_bet, e_wl, e_bl, e_wr, e_br, e_wo, e_bo,
     m_gam, m_bet, m_wl, m_bl, m_wr, m_br, m_wo, m_bo,
     pair_out, e_t, m_out, e_out, e_half,
@@ -76,6 +84,8 @@
     def rblk(d, n=rows):
         return part(d, n)
 
+    for copy in copies:
+        copy.start()
     barrier = pltpu.get_barrier_semaphore()
     for k in range(1, 8):
         pl.semaphore_signal(barrier, inc=1, device_id=dev(partner(me, k)), device_id_type=pl.DeviceIdType.MESH)
@@ -100,6 +110,9 @@
     def row_of(ref):
         v = ref[:].astype(F32)
         return v.reshape(1, v.shape[0])
+
+    for copy in copies:
+        copy.wait()
 
     def weights(wf, wp):
         gam_e[:] = column(row_of(e_gam), HALF, 1)
@@ -624,8 +637,11 @@
 
 def store_kernel(pair_in, e_in, m_in, pair_out, e_out, m_out, sem):
     copies = []
-    for i, (src, dst) in enumerate(((pair_in, pair_out), (e_in, e_out), (m_in, m_out))):
-        copies.append(pltpu.make_async_copy(src, dst, sem.at[i]))
+    for src, dst, pieces in ((e_in, e_out, 6), (pair_in, pair_out, 2), (m_in, m_out, 2)):
+        n = src.shape[0] // pieces
+        for i in range(pieces):
+            at = pl.ds(i * n, n)
+            copies.append(pltpu.make_async_copy(src.at[at], dst.at[at], sem.at[len(copies)]))
     for copy in copies:
         copy.start()
     for copy in copies:
@@ -647,7 +663,7 @@
         nk = e_wo.shape[1]
         seq = seqs // 8
         args = (
-            jnp.transpose(extra_block, (1, 2, 0)), main_block, extra_mask, main_mask, pair_rows,
+            jnp.transpose(extra_block, (1, 2, 0)), main_block, extra_mask, pair_rows, main_mask,
             e_gam, e_bet, e_wl.T, e_bl, e_wr.T, e_br, e_wo, e_bo, m_gam, m_bet, m_wl.T, m_bl, m_wr.T, m_br, m_wo, m_bo)
         any_spec = pl.BlockSpec(memory_space=pl.ANY)
         vmem = pl.BlockSpec(memory_space=pltpu.VMEM)
@@ -660,9 +676,9 @@
                 pltpu.VMEM((mseqs // 8, res, cm), BF),
                 jax.ShapeDtypeStruct((res, ce, seq), BF),
                 jax.ShapeDtypeStruct((seq, ce, res // 2), BF)),
-            in_specs=[any_spec, any_spec, any_spec, vmem, any_spec] + [vmem] * 16,
+            in_specs=[any_spec] * 4 + [pl.BlockSpec(memory_space=pltpu.HBM)] * SMALL,
             out_specs=(vmem, vmem, vmem, any_spec, any_spec),
-            scratch_shapes=[
+            scratch_shapes=[pltpu.VMEM(x.shape, x.dtype) for x in args[4:]] + [
                 pltpu.VMEM((4 * rows * hid, 2 * seq), BF),
                 pltpu.VMEM((4 * rows * hid, seq), BF),
                 pltpu.VMEM((rows, ce, seq), BF),
@@ -693,7 +709,7 @@
                 dma((8,)), dma((8,)), dma((8,)), dma((8,)), dma((4, 3)), dma((4, 3)), dma((8, 3)), dma((8, 3)),
                 dma((2,)), dma((2,)), dma((2,)), dma((2,)),
                 dma((3,)), dma((3,)), dma((3,)), dma((3,)), dma((8,)), dma((8,)),
-                dma((8,)), dma((8,)), pltpu.SemaphoreType.REGULAR, dma((8,))],
+                dma((8,)), dma((8,)), pltpu.SemaphoreType.REGULAR, dma((8,)), dma((SMALL,))],
             compiler_params=pltpu.CompilerParams(
                 collective_id=0, has_side_effects=True, vmem_limit_bytes=VMEM_LIMIT),
             name='opm',
@@ -703,7 +719,7 @@
             out_shape=tuple(jax.ShapeDtypeStruct(x.shape, x.dtype) for x in (pair_out, e_seq, m_seq)),
             in_specs=[vmem] * 3,
             out_specs=(any_spec,) * 3,
-            scratch_shapes=[dma((3,))],
+            scratch_shapes=[dma((10,))],
             compiler_params=pltpu.CompilerParams(vmem_limit_bytes=2 ** 20),
             name='store',
         )(pair_out, e_seq, m_seq)

time: 271 us -> 270 us (level)
  no operation moved by 1% of the time
where the time goes in v8:
time: 270 us; the launch traced here: 269 us
  Pallas kernels  268 us (99%)
    pallas_call x1, Pallas kernels, local_program(): pl.pallas_call(opm_kernel, out_shape=(pltpu.VMEM((rows, res, nk), F32), p...  261 us
    pallas_call x1, Pallas kernels, local_program(): pl.pallas_call(store_kernel, out_shape=tuple((jax.ShapeDtypeStruct(x.shap...  7.2 us

profile of v8, /device:TPU:0, one launch (start us, length us, event | category | flops | bytes accessed | tf_op | source)
XLA Modules:
  0.0 269.0 jit_solution(2677170728598049225)
XLA Ops:
  0.6 261.1 %opm.1 = (f32[32,256,128]{2,1,0:T(8,128)S(1)}, bf16[384,64,256]{2,1,0:T(8,128)(2,1)S(1)}, bf16[32,256,256]{2,1,0:T(8,128)(2,1)S(1)}, bf16[256,64,384]{2,1,0:T(8,128)(2,1)}, bf16[384,64,128]{2,1,0:T(8,128)(2,1)}) custom-call(bf16[32,64,3072]{2,1,0:T(8,128)(2,1)} %bitcast.6, bf16[256,32,256]{2,1,0:T(8,128)(2,1)} %xm.1, s32[3072,256]{1,0:T(8,128)} %mask_e.1, ...), custom_call_target="tpu_custom_call" | custom-call | tf_op jit(solution)/shard_map/opm/pallas_call | solution.py:671
  261.8 7.2 %store.1 = (f32[32,256,128]{2,1,0:T(8,128)}, bf16[384,64,256]{2,1,0:T(8,128)(2,1)}, bf16[32,256,256]{2,1,0:T(8,128)(2,1)}) custom-call(f32[32,256,128]{2,1,0:T(8,128)S(1)} %get-tuple-element.9.pair_in, bf16[384,64,256]{2,1,0:T(8,128)(2,1)S(1)} %get-tuple-element.10.e_in, bf16[32,256,256]{2,1,0:T(8,128)(2,1)S(1)} %get-tuple-element.11.m_in), custom_call_target="tpu_custom_call" | custom-call | tf_op jit(solution)/shard_map/store/pallas_call | solution.py:717

commit v9 on v8

--- a/solution.py
+++ b/solution.py
@@ -226,7 +226,7 @@
 
     for i in range(3):
         g_copy(i).start()
-    for k in (1, 2, 4):
+    for k in (1, 2, 4, 3, 5):
         m_copy(k).start()
 
     def project(hh, m16):
@@ -542,7 +542,7 @@
                             d_copy(i).start()
                             f_copy(i).start()
                     if v == 1:
-                        for k in (3, 5, 6, 7):
+                        for k in (6, 7):
                             m_copy(k).start()
         loop(8, eblk)
 

time: 270 us -> 280 us (1.037)
  Pallas kernels: 268 us -> 277 us
    pallas_call x1, Pallas kernels: 261 us -> 270 us  [local_program(): pl.pallas_call(opm_kernel, out_shape=(pltpu.VMEM((rows, res, nk), F32), p...]
where the time goes in v9:
time: 280 us; the launch traced here: 278 us
  Pallas kernels  277 us (99%)
    pallas_call x1, Pallas kernels, local_program(): pl.pallas_call(opm_kernel, out_shape=(pltpu.VMEM((rows, res, nk), F32), p...  270 us
    pallas_call x1, Pallas kernels, local_program(): pl.pallas_call(store_kernel, out_shape=tuple((jax.ShapeDtypeStruct(x.shap...  7.2 us

profile of v9, /device:TPU:0, one launch (start us, length us, event | category | flops | bytes accessed | tf_op | source)
XLA Modules:
  0.0 277.6 jit_solution(11426230255345129080)
XLA Ops:
  0.6 269.8 %opm.1 = (f32[32,256,128]{2,1,0:T(8,128)S(1)}, bf16[384,64,256]{2,1,0:T(8,128)(2,1)S(1)}, bf16[32,256,256]{2,1,0:T(8,128)(2,1)S(1)}, bf16[256,64,384]{2,1,0:T(8,128)(2,1)}, bf16[384,64,128]{2,1,0:T(8,128)(2,1)}) custom-call(bf16[32,64,3072]{2,1,0:T(8,128)(2,1)} %bitcast.6, bf16[256,32,256]{2,1,0:T(8,128)(2,1)} %xm.1, s32[3072,256]{1,0:T(8,128)} %mask_e.1, ...), custom_call_target="tpu_custom_call" | custom-call | tf_op jit(solution)/shard_map/opm/pallas_call | solution.py:671
  270.4 7.2 %store.1 = (f32[32,256,128]{2,1,0:T(8,128)}, bf16[384,64,256]{2,1,0:T(8,128)(2,1)}, bf16[32,256,256]{2,1,0:T(8,128)(2,1)}) custom-call(f32[32,256,128]{2,1,0:T(8,128)S(1)} %get-tuple-element.9.pair_in, bf16[384,64,256]{2,1,0:T(8,128)(2,1)S(1)} %get-tuple-element.10.e_in, bf16[32,256,256]{2,1,0:T(8,128)(2,1)S(1)} %get-tuple-element.11.m_in), custom_call_target="tpu_custom_call" | custom-call | tf_op jit(solution)/shard_map/store/pallas_call | solution.py:717
